TPU v7x, 256 devices: a whole 4x4x8 slice. The times are simulated.
256 devices in a mesh: seq: 32 (over z, y), blk: 8 (over x, core).
Axes of the slice: x: 4, y: 4, z: 8, core: 2. Of those that a mesh axis runs over, the one named last changes fastest.
Arguments:
- q_latent: bfloat16 [64, 128, 512], P('blk', 'seq'), may hold values from -16 to 16
- q_rope: bfloat16 [64, 64, 128], P('blk', None, 'seq'), may hold values from -9 to 9
- cache_latent: bfloat16 [131072, 512], P(('seq', 'blk')), may hold values from -8 to 8
- cache_rope: bfloat16 [64, 131072], P(None, ('seq', 'blk')), may hold values from -6 to 6
- draft_latent: bfloat16 [64, 512], replicated, may hold values from -8 to 8
- draft_rope: bfloat16 [64, 64], replicated, may hold values from -6 to 6
- ancestors: int32 [64, 64], replicated, may hold values from 0 to 1, as said below
- valid_length: int32 [], replicated, may hold values from 65536 to 131072
- accepted: int32 [64], P('blk'), may hold values from 0 to 1, as said below
- w_value: bfloat16 [128, 512, 128], P('seq'), may hold values from -3 to 3
Outputs:
- attended: bfloat16 [64, 128, 128], P('blk', 'seq')
- accepted_total: int32 [], replicated
Inputs may be any that keep to these rules, and one draw needn't show every extreme that they name: Node 0 is the root; every other node's parent has a lower index; ancestors[i, j] = 1 exactly when j is i or an ancestor of i. accepted is the row of ancestors of one node of the tree: that node and all of its ancestors.
All inputs are finite; a program needn't handle non-finite values.
Results may differ from a plain program's by a relative error of at most 0.02.
Values may be sent and summed in bfloat16 or wider, within the bound.
No kernel may reach another device: no remote copies, remote signals or barrier semaphores. Data moves between devices by JAX's collectives and lax.ppermute only.
A program may use at most 64 MiB of HBM per device.

v0:
```python
import functools
import math

import jax
import jax.numpy as jnp
from jax import lax
from jax.experimental import pallas as pl
from jax.experimental.pallas import tpu as pltpu
from jax.sharding import Mesh
from jax.sharding import PartitionSpec as P

ROPE = 64
VDIM = 128
LATENT = 512
LANES = 128
SEQ = ("z", "y")
BLK = ("x", "core")
NEG = -1e30
SCALE2 = (VDIM + ROPE) ** -0.5 * math.log2(math.e)

ROWS = 32
Q_ROWS = 144
O_ROWS = 136
OWNERS = 8
EXTRA = 8
BLOCK = OWNERS * ROWS


def dot(a, b, contract=((1,), (0,))):
    return lax.dot_general(a, b, (contract, ((), ())), preferred_element_type=jnp.float32)


def three_parts(value):
    high = value.astype(jnp.bfloat16)
    rest = value - high.astype(jnp.float32)
    middle = rest.astype(jnp.bfloat16)
    low = (rest - middle.astype(jnp.float32)).astype(jnp.bfloat16)
    return high, middle, low


def attend_kernel(n_queries, n_chunks, *refs):
    q_refs, chunks = refs[:n_queries], refs[n_queries : n_queries + n_chunks]
    out_ref, count_ref, query, query_rope, scores = refs[n_queries + n_chunks :]
    rows = LATENT
    lane = lax.broadcasted_iota(jnp.int32, (BLOCK, LANES), 1)
    query_rope[...] = jnp.where(lane == ROPE, 1.0, 0.0).astype(jnp.bfloat16)
    own_lane = lax.broadcasted_iota(jnp.int32, (ROWS, LANES), 1)
    own_row = lax.broadcasted_iota(jnp.int32, (ROWS, LANES), 0)
    count = jnp.zeros((EXTRA, LANES), jnp.float32)
    for c in range(n_chunks):
        count = count + chunks[c][rows + ROPE :, :LANES].astype(jnp.float32)
    count_ref[...] = count
    owners = [q_ref.at[i] for q_ref in q_refs for i in range(q_ref.shape[0])]
    for i in range(OWNERS):
        for j in range(4):
            query[i * ROWS : (i + 1) * ROWS, j * LANES : (j + 1) * LANES] = owners[i][
                j * ROWS : (j + 1) * ROWS, :
            ]
        both = owners[i][4 * ROWS :, :]
        query_rope[i * ROWS : i * ROWS + 16, :ROPE] = both[:, :ROPE]
        query_rope[i * ROWS + 16 : (i + 1) * ROWS, :ROPE] = both[:, ROPE:]
    peak = None
    for c in range(n_chunks):
        here = slice(c * rows, (c + 1) * rows)
        s = dot(query[...], chunks[c][:rows, :], ((1,), (1,)))
        s = s + dot(query_rope[:, : ROPE + EXTRA], chunks[c][rows:, :])
        scores[:, here] = s
        for j in range(rows // LANES):
            part = s[:, j * LANES : (j + 1) * LANES]
            peak = part if peak is None else jnp.maximum(peak, part)
    peak = jnp.max(peak, axis=1, keepdims=True)
    total = jnp.zeros((BLOCK, LANES), jnp.float32)
    latent = jnp.zeros((BLOCK, LATENT), jnp.float32)
    for c in range(n_chunks):
        here = slice(c * rows, (c + 1) * rows)
        p = jnp.exp2((scores[:, here] - peak) * SCALE2)
        for j in range(rows // LANES):
            total = total + p[:, j * LANES : (j + 1) * LANES]
        latent = latent + dot(p.astype(jnp.bfloat16), chunks[c][:rows, :])
    total = jnp.sum(total, axis=1, keepdims=True)
    latent = (latent * (1.0 / total)).astype(jnp.bfloat16)
    lse = peak * SCALE2 + jnp.log2(total)
    for i in range(OWNERS):
        mine = slice(i * ROWS, (i + 1) * ROWS)
        for j in range(4):
            out_ref[i, j * ROWS : (j + 1) * ROWS, :] = latent[mine, j * LANES : (j + 1) * LANES]
        line = jnp.where(own_lane == own_row, lse[mine, :], 0.0)
        out_ref[i, 4 * ROWS :, :] = lines_of(jnp.sum(line, axis=0, keepdims=True))


def lines_of(line):
    parts = [p.astype(jnp.float32) for p in three_parts(line)]
    pad = jnp.zeros((EXTRA - 3, LANES), jnp.float32)
    return jnp.concatenate(parts + [pad], axis=0).astype(jnp.bfloat16)


def attend(queries, chunks):
    vmem = pl.BlockSpec(memory_space=pltpu.VMEM)
    n = len(chunks)
    return pl.pallas_call(
        functools.partial(attend_kernel, len(queries), n),
        out_shape=(
            jax.ShapeDtypeStruct((OWNERS, O_ROWS, LANES), jnp.bfloat16),
            jax.ShapeDtypeStruct((EXTRA, LANES), jnp.float32),
        ),
        in_specs=[vmem] * (len(queries) + n),
        out_specs=(vmem, vmem),
        scratch_shapes=[
            pltpu.VMEM((BLOCK, LATENT), jnp.bfloat16),
            pltpu.VMEM((BLOCK, LANES), jnp.bfloat16),
            pltpu.VMEM((BLOCK, n * LATENT), jnp.float32),
        ],
        compiler_params=pltpu.CompilerParams(vmem_limit_bytes=12 * 2**20),
        cost_estimate=pl.CostEstimate(
            flops=BLOCK * n * LATENT * 2 * 1280, bytes_accessed=2**20, transcendentals=0
        ),
        name="attend",
    )(*queries, *chunks)


def merge_kernel(*refs):
    pieces, out_ref = refs[:-1], refs[-1]
    own_lane = lax.broadcasted_iota(jnp.int32, (ROWS, LANES), 1)
    diagonal = own_lane == lax.broadcasted_iota(jnp.int32, (ROWS, LANES), 0)
    for i in range(out_ref.shape[0]):
        lses = []
        for piece in pieces:
            parts = piece[i, 4 * ROWS :, :].astype(jnp.float32)
            lses.append(parts[0:1, :] + parts[1:2, :] + parts[2:3, :])
        peak = functools.reduce(jnp.maximum, lses)
        shares = [jnp.exp2(lse - peak) for lse in lses]
        total = sum(shares[1:], shares[0])
        out_ref[i, 4 * ROWS :, :] = lines_of(peak + jnp.log2(total))
        shares = [
            jnp.sum(jnp.where(diagonal, share / total, 0.0), axis=1, keepdims=True)
            for share in shares
        ]
        for j in range(4):
            mine = slice(j * ROWS, (j + 1) * ROWS)
            latent = sum(p[i, mine, :].astype(jnp.float32) * s for p, s in zip(pieces, shares))
            out_ref[i, mine, :] = latent.astype(jnp.bfloat16)


def merge(pieces):
    vmem = pl.BlockSpec(memory_space=pltpu.VMEM)
    return pl.pallas_call(
        merge_kernel,
        out_shape=jax.ShapeDtypeStruct(pieces[0].shape, pieces[0].dtype),
        in_specs=[vmem] * len(pieces),
        out_specs=vmem,
        compiler_params=pltpu.CompilerParams(vmem_limit_bytes=8 * 2**20),
        name="merge",
    )(*pieces)


def pack_query_kernel(lat_ref, rope_ref, out_ref, packed):
    tokens, heads = lat_ref.shape[:2]
    for t in range(tokens):
        lat = lat_ref[t].astype(jnp.float32)
        for j in range(4):
            first = j * ROWS + t * heads
            packed[first : first + heads, :] = lat[:, j * LANES : (j + 1) * LANES]
        first = 4 * ROWS + (t % (tokens // 2)) * heads
        side = (t // (tokens // 2)) * ROPE
        packed[first : first + heads, side : side + ROPE] = rope_ref[t].astype(jnp.float32)
    block = packed[...].astype(jnp.bfloat16)
    for i in range(out_ref.shape[0]):
        out_ref[i] = block


def pack_query(q_latent, q_rope, copies):
    vmem = pl.BlockSpec(memory_space=pltpu.VMEM)
    return pl.pallas_call(
        pack_query_kernel,
        out_shape=jax.ShapeDtypeStruct((copies, Q_ROWS, LANES), jnp.bfloat16),
        in_specs=[vmem] * 2,
        out_specs=vmem,
        scratch_shapes=[pltpu.VMEM((Q_ROWS, LANES), jnp.float32)],
        compiler_params=pltpu.CompilerParams(vmem_limit_bytes=8 * 2**20),
        name="pack_query",
    )(q_latent, q_rope)


def pack_cache_kernel(valid_ref, accepted_ref, lat_ref, rope_ref, out_ref):
    limit = valid_ref[0] - lax.axis_index(SEQ + BLK) * LATENT
    count = sum(accepted_ref[i] for i in range(accepted_ref.shape[0]))
    out_ref[:LATENT, :] = lat_ref[...]
    out_ref[LATENT : LATENT + ROPE, :] = rope_ref[...]
    lane = lax.broadcasted_iota(jnp.int32, (EXTRA, LATENT), 1)
    row = lax.broadcasted_iota(jnp.int32, (EXTRA, LATENT), 0)
    dead = jnp.where((row == 0) & (lane >= limit), NEG, 0.0)
    extra = jnp.where(row == 1, count.astype(jnp.float32), dead)
    out_ref[LATENT + ROPE :, :] = extra.astype(jnp.bfloat16)


def pack_cache(valid_length, accepted, cache_latent, cache_rope):
    vmem = pl.BlockSpec(memory_space=pltpu.VMEM)
    smem = pl.BlockSpec(memory_space=pltpu.SMEM)
    return pl.pallas_call(
        pack_cache_kernel,
        out_shape=jax.ShapeDtypeStruct((LATENT + ROPE + EXTRA, LATENT), jnp.bfloat16),
        in_specs=[smem, smem, vmem, vmem],
        out_specs=vmem,
        compiler_params=pltpu.CompilerParams(vmem_limit_bytes=8 * 2**20),
        name="pack_cache",
    )(valid_length.reshape(1), accepted, cache_latent, cache_rope)


def finish_kernel(tokens, heads, pieces_ref, q_ref, d_lat_ref, d_rope_ref, tree_ref, w_ref, out_ref):
    n = pieces_ref.shape[0]
    parts = pieces_ref[:, 4 * ROWS :, :].astype(jnp.float32)
    lse = parts[:, 0, :] + parts[:, 1, :] + parts[:, 2, :]
    query = jnp.concatenate([q_ref[j * ROWS : (j + 1) * ROWS, :] for j in range(4)], axis=1)
    both = q_ref[4 * ROWS :, :]
    query_rope = jnp.concatenate([both[:, :ROPE], both[:, ROPE:]], axis=0)
    draft = d_lat_ref[...]
    score = dot(query, draft, ((1,), (1,))) + dot(query_rope, d_rope_ref[...])
    score = jnp.where(tree_ref[...] == 1, score * SCALE2, NEG)
    draft_peak = jnp.max(score, axis=1, keepdims=True)
    own_lane = lax.broadcasted_iota(jnp.int32, (ROWS, LANES), 1)
    own_row = lax.broadcasted_iota(jnp.int32, (ROWS, LANES), 0)
    diagonal = own_lane == own_row

    def to_rows(line):
        return jnp.sum(jnp.where(diagonal, line, 0.0), axis=1, keepdims=True)

    cache_peak = to_rows(jnp.max(lse, axis=0, keepdims=True))
    peak = jnp.maximum(cache_peak, draft_peak)
    weight = jnp.exp2(score - peak)
    total = jnp.sum(weight, axis=1, keepdims=True)
    latent = dot(weight.astype(jnp.bfloat16), draft)
    for i in range(n):
        share = jnp.exp2(to_rows(lse[i : i + 1, :]) - peak)
        total = total + share
        piece = jnp.concatenate(
            [pieces_ref[i, j * ROWS : (j + 1) * ROWS, :] for j in range(4)], axis=1
        )
        latent = latent + share * piece.astype(jnp.float32)
    latent = latent / total
    high = latent.astype(jnp.bfloat16)
    low = (latent - high.astype(jnp.float32)).astype(jnp.bfloat16)
    head = lax.broadcasted_iota(jnp.int32, (ROWS, VDIM), 0) % heads
    value = jnp.zeros((ROWS, VDIM), jnp.float32)
    for h in range(heads):
        value = jnp.where(head == h, dot(high, w_ref[h]) + dot(low, w_ref[h]), value)
    for t in range(tokens):
        out_ref[t] = value[t * heads : (t + 1) * heads, :].astype(out_ref.dtype)


def finish(pieces, own, draft_latent, draft_rope, tree, w_value, tokens, heads):
    vmem = pl.BlockSpec(memory_space=pltpu.VMEM)
    return pl.pallas_call(
        functools.partial(finish_kernel, tokens, heads),
        out_shape=jax.ShapeDtypeStruct((tokens, heads, VDIM), jnp.bfloat16),
        in_specs=[vmem] * 6,
        out_specs=vmem,
        compiler_params=pltpu.CompilerParams(vmem_limit_bytes=8 * 2**20),
        name="finish",
    )(pieces, own, draft_latent, draft_rope, tree, w_value)


def both_ways(n, step):
    return [
        (i * 2 + core, (i + (step if core == 0 else -step)) % n * 2 + core)
        for i in range(n)
        for core in range(2)
    ]


def shift(value, axis, step):
    return lax.ppermute(value, (axis, "core"), both_ways(lax.axis_size(axis), step))


def across(value, axis):
    n = lax.axis_size(axis)
    return lax.ppermute(value, axis, [(i, (i + n // 2) % n) for i in range(n)])


def other_core(value):
    return lax.ppermute(value, "core", [(0, 1), (1, 0)])


def shards(
    q_latent,
    q_rope,
    cache_latent,
    cache_rope,
    draft_latent,
    draft_rope,
    ancestors,
    valid_length,
    accepted,
    w_value,
):
    tokens, heads = q_latent.shape[:2]
    nz = lax.axis_size("z")

    packed = pack_query(q_latent, q_rope.transpose(0, 2, 1), nz)
    own = pack_cache(valid_length, accepted, cache_latent, cache_rope)
    ahead = shift(own, "x", 1)
    behind = shift(own, "x", -1)
    far = shift(ahead, "x", 1)
    near = lax.all_to_all(packed, "z", 0, 0, tiled=True)
    q_far = across(near, "y")
    q_ahead = shift(near, "y", 1)
    q_behind = shift(near, "y", -1)
    mine = (own, ahead, behind, far)
    chunks = list(mine)
    for chunk in mine:
        chunks.append(other_core(chunk))

    part_far, counts = attend((q_far,), chunks)
    part_ahead, _ = attend((q_ahead,), chunks)
    part_behind, _ = attend((q_behind,), chunks)
    part_near, _ = attend((near,), chunks)
    from_far = across(part_far, "y")
    from_ahead = shift(part_ahead, "y", -1)
    from_behind = shift(part_behind, "y", 1)
    pieces = merge((part_near, from_far, from_ahead, from_behind))
    pieces = lax.all_to_all(pieces, "z", 0, 0, tiled=True)
    tree = lax.dynamic_slice_in_dim(ancestors, lax.axis_index(BLK) * tokens, tokens, 0)
    tree = jnp.repeat(tree, heads, axis=0)
    attended = finish(pieces, packed[0], draft_latent, draft_rope, tree, w_value, tokens, heads)
    return (attended, counts[1, 0].astype(jnp.int32))


def solution(mesh):
    finer = Mesh(mesh.devices.reshape(8, 4, 4, 2), SEQ + BLK)

    return jax.shard_map(
        shards,
        mesh=finer,
        in_specs=(
            P(BLK, SEQ, None),
            P(BLK, None, SEQ),
            P(SEQ + BLK, None),
            P(None, SEQ + BLK),
            P(),
            P(),
            P(),
            P(),
            P(BLK),
            P(SEQ, None, None),
        ),
        out_specs=(P(BLK, SEQ, None), P()),
        check_vma=False,
    )
```

profile of v0, /device:TPU:24, one launch (start us, length us, event | category | flops | bytes accessed | tf_op | source)
XLA Modules:
  0.0 100.3 jit_solution(17513414931926259233)
XLA Ops:
  0.6 0.0 copy-start
  1.3 0.6 copy-done.8
  2.0 1.0 %copy-done.1 = bf16[512,512]{1,0:T(8,128)(2,1)S(1)} copy-done((bf16[512,512]{1,0:T(8,128)(2,1)S(1)}, bf16[512,512]{1,0:T(8,128)(2,1)}, u32[]{:S(2)}) %copy-start.1) | copy-done | bytes 524312
  3.0 0.8 copy-done.3
  3.8 0.6 pack_cache.1.refs_1_
  4.4 1.6 %collective-permute-start = (bf16[584,512]{1,0:T(8,128)(2,1)S(1)}, bf16[584,512]{1,0:T(8,128)(2,1)S(1)}, u32[]{:S(2)}, u32[]{:S(2)}) collective-permute-start(bf16[584,512]{1,0:T(8,128)(2,1)S(1)} %pack_cache.1.refs_1_), channel_id=1, source_target_pairs={{0,2},{1,7},{2,4},{3,1},{4,6},{5,3},{6,0},{7,5},{8,10},{9,15},{10,... | collective-permute-start | bytes 1794056 | tf_op jit(solution)/shard_map/ppermute | solution.py:271
  6.0 1.7 %collective-permute-start.1 = (bf16[584,512]{1,0:T(8,128)(2,1)S(1)}, bf16[584,512]{1,0:T(8,128)(2,1)S(1)}, u32[]{:S(2)}, u32[]{:S(2)}) collective-permute-start(bf16[584,512]{1,0:T(8,128)(2,1)S(1)} %pack_cache.1.refs_1_), channel_id=1, source_target_pairs={{0,6},{1,3},{2,0},{3,5},{4,2},{5,7},{6,4},{7,1},{8,14},{9,11},{10,... | collective-permute-start | bytes 1794056 | tf_op jit(solution)/shard_map/ppermute | solution.py:271
  7.7 13.0 %collective-permute-done.refs_2_ = bf16[584,512]{1,0:T(8,128)(2,1)S(1)} collective-permute-done((bf16[584,512]{1,0:T(8,128)(2,1)S(1)}, bf16[584,512]{1,0:T(8,128)(2,1)S(1)}, u32[]{:S(2)}, u32[]{:S(2)}) %collective-permute-start) | collective-permute-done | bytes 598048 | tf_op jit(solution)/shard_map/ppermute | solution.py:271
  20.8 1.5 %collective-permute-start.2 = (bf16[584,512]{1,0:T(8,128)(2,1)S(1)}, bf16[584,512]{1,0:T(8,128)(2,1)S(1)}, u32[]{:S(2)}, u32[]{:S(2)}) collective-permute-start(bf16[584,512]{1,0:T(8,128)(2,1)S(1)} %collective-permute-done.refs_2_), channel_id=1, source_target_pairs={{0,2},{1,7},{2,4},{3,1},{4,6},{5,3},{6,0},{7,5},{8,10},{9,15},{10,... | collective-permute-start | bytes 1794056 | tf_op jit(solution)/shard_map/ppermute | solution.py:271
  22.2 0.8 pack_query.1
  23.0 8.5 %all-to-all-start = ((bf16[8,144,128]{2,1,0:T(8,128)(2,1)}), bf16[8,144,128]{2,1,0:T(8,128)(2,1)S(1)}, u32[]{:S(2)}, u32[]{:S(2)}) async-start(bf16[8,144,128]{2,1,0:T(8,128)(2,1)} %pack_query.1), calls=%async_computation | async-start | bytes 589824 | tf_op jit(solution)/shard_map/all_to_all | solution.py:303
  31.5 0.5 collective-permute-start.4
  32.0 0.1 collective-permute-start.5
  32.1 0.4 collective-permute-start.6
  32.5 11.4 %all-to-all-done.refs_0_ = bf16[8,144,128]{2,1,0:T(8,128)(2,1)S(1)} async-done(((bf16[8,144,128]{2,1,0:T(8,128)(2,1)}), bf16[8,144,128]{2,1,0:T(8,128)(2,1)S(1)}, u32[]{:S(2)}, u32[]{:S(2)}) %all-to-all-start) | async-done | bytes 294944 | tf_op jit(solution)/shard_map/all_to_all | solution.py:303
  44.0 1.2 %collective-permute-start.7 = (bf16[8,144,128]{2,1,0:T(8,128)(2,1)S(1)}, bf16[8,144,128]{2,1,0:T(8,128)(2,1)S(1)}, u32[]{:S(2)}, u32[]{:S(2)}) collective-permute-start(bf16[8,144,128]{2,1,0:T(8,128)(2,1)S(1)} %all-to-all-done.refs_0_), channel_id=1, source_target_pairs={{0,16},{8,24},{16,0},{24,8},{1,17},{9,25},{17,1},{25,9},{2,18},{10... | collective-permute-start | bytes 884744 | tf_op jit(solution)/shard_map/ppermute | solution.py:276
  45.2 7.9 %collective-permute-done.7.refs_0_ = bf16[8,144,128]{2,1,0:T(8,128)(2,1)S(1)} collective-permute-done((bf16[8,144,128]{2,1,0:T(8,128)(2,1)S(1)}, bf16[8,144,128]{2,1,0:T(8,128)(2,1)S(1)}, u32[]{:S(2)}, u32[]{:S(2)}) %collective-permute-start.7) | collective-permute-done | bytes 294944 | tf_op jit(solution)/shard_map/ppermute | solution.py:276
  53.1 2.5 %collective-permute-start.9 = (bf16[8,144,128]{2,1,0:T(8,128)(2,1)S(1)}, bf16[8,144,128]{2,1,0:T(8,128)(2,1)S(1)}, u32[]{:S(2)}, u32[]{:S(2)}) collective-permute-start(bf16[8,144,128]{2,1,0:T(8,128)(2,1)S(1)} %all-to-all-done.refs_0_), channel_id=1, source_target_pairs={{0,8},{1,25},{8,16},{9,1},{16,24},{17,9},{24,0},{25,17},{2,10},{3,... | collective-permute-start | bytes 884744 | tf_op jit(solution)/shard_map/ppermute | solution.py:271
  55.6 4.9 %attend.5 = (bf16[8,136,128]{2,1,0:T(8,128)(2,1)S(1)}, f32[8,128]{1,0:T(8,128)S(1)}) custom-call(bf16[8,144,128]{2,1,0:T(8,128)(2,1)S(1)} %collective-permute-done.7.refs_0_, bf16[584,512]{1,0:T(8,128)(2,1)S(1)} %pack_cache.1.refs_1_, bf16[584,512]{1,0:T(8,128)(2,1)S(1)} %collective-permute-done.refs_2_, ...), custom_call_target="tpu_custom_call" | custom-call | flops 2684354560 | bytes 1048576 | tf_op jit(solution)/shard_map/attend/pallas_call | solution.py:100
  60.5 2.9 %collective-permute-start.8 = (bf16[8,136,128]{2,1,0:T(8,128)(2,1)S(1)}, bf16[8,136,128]{2,1,0:T(8,128)(2,1)S(1)}, u32[]{:S(2)}, u32[]{:S(2)}) collective-permute-start(bf16[8,136,128]{2,1,0:T(8,128)(2,1)S(1)} %get-tuple-element.8), channel_id=1, source_target_pairs={{0,16},{8,24},{16,0},{24,8},{1,17},{9,25},{17,1},{25,9},{2,18},{10... | collective-permute-start | bytes 835592 | tf_op jit(solution)/shard_map/ppermute | solution.py:276
  63.4 5.5 %attend.7 = (bf16[8,136,128]{2,1,0:T(8,128)(2,1)S(1)}, f32[8,128]{1,0:T(8,128)}) custom-call(bf16[8,144,128]{2,1,0:T(8,128)(2,1)S(1)} %collective-permute-done.11.refs_0_, bf16[584,512]{1,0:T(8,128)(2,1)S(1)} %pack_cache.1.refs_1_, bf16[584,512]{1,0:T(8,128)(2,1)S(1)} %collective-permute-done.refs_2_, bf16[584,512]{1,0:T(8,128)(2,1)S(1)} %collective-permute-done.1.refs_3_, ...), custom_call_target="tpu_custom_call" | custom-call | flops 2684354560 | bytes 1048576 | tf_op jit(solution)/shard_map/attend/pallas_call | solution.py:100
  68.8 0.6 collective-permute-start.12
  69.5 5.5 %attend.6 = (bf16[8,136,128]{2,1,0:T(8,128)(2,1)S(1)}, f32[8,128]{1,0:T(8,128)}) custom-call(bf16[8,144,128]{2,1,0:T(8,128)(2,1)S(1)} %collective-permute-done.9.refs_0_, bf16[584,512]{1,0:T(8,128)(2,1)S(1)} %pack_cache.1.refs_1_, bf16[584,512]{1,0:T(8,128)(2,1)S(1)} %collective-permute-done.refs_2_, bf16[584,512]{1,0:T(8,128)(2,1)S(1)} %collective-permute-done.1.refs_3_, ...), custom_call_target="tpu_custom_call" | custom-call | flops 2684354560 | bytes 1048576 | tf_op jit(solution)/shard_map/attend/pallas_call | solution.py:100
  74.9 1.4 %collective-permute-start.10 = (bf16[8,136,128]{2,1,0:T(8,128)(2,1)S(1)}, bf16[8,136,128]{2,1,0:T(8,128)(2,1)S(1)}, u32[]{:S(2)}, u32[]{:S(2)}) collective-permute-start(bf16[8,136,128]{2,1,0:T(8,128)(2,1)S(1)} %get-tuple-element.9), channel_id=1, source_target_pairs={{0,24},{1,9},{8,0},{9,17},{16,8},{17,25},{24,16},{25,1},{2,26},{3,... | collective-permute-start | bytes 835592 | tf_op jit(solution)/shard_map/ppermute | solution.py:271
  76.3 5.5 %attend.4 = (bf16[8,136,128]{2,1,0:T(8,128)(2,1)S(1)}, f32[8,128]{1,0:T(8,128)}) custom-call(bf16[8,144,128]{2,1,0:T(8,128)(2,1)S(1)} %all-to-all-done.refs_0_, bf16[584,512]{1,0:T(8,128)(2,1)S(1)} %pack_cache.1.refs_1_, bf16[584,512]{1,0:T(8,128)(2,1)S(1)} %collective-permute-done.refs_2_, bf16[584,512]{1,0:T(8,128)(2,1)S(1)} %collective-permute-done.1.refs_3_, ...), custom_call_target="tpu_custom_call" | custom-call | flops 2684354560 | bytes 1048576 | tf_op jit(solution)/shard_map/attend/pallas_call | solution.py:100
  81.8 0.9 collective-permute-done.10.refs_2_
  82.7 1.0 %merge.1 = bf16[8,136,128]{2,1,0:T(8,128)(2,1)} custom-call(bf16[8,136,128]{2,1,0:T(8,128)(2,1)S(1)} %get-tuple-element.7.refs_0_, bf16[8,136,128]{2,1,0:T(8,128)(2,1)S(1)} %collective-permute-done.8.refs_1_, bf16[8,136,128]{2,1,0:T(8,128)(2,1)S(1)} %collective-permute-done.10.refs_2_, bf16[8,136,128]{2,1,0:T(8,128)(2,1)S(1)} %collective-permute-done.12.refs_3_), custom_call_target="tpu_custom_call" | custom-call | tf_op jit(solution)/shard_map/merge/pallas_call | solution.py:146
  83.7 3.5 %all-to-all-start.1 = ((bf16[8,136,128]{2,1,0:T(8,128)(2,1)}), bf16[8,136,128]{2,1,0:T(8,128)(2,1)S(1)}, u32[]{:S(2)}, u32[]{:S(2)}) async-start(bf16[8,136,128]{2,1,0:T(8,128)(2,1)} %merge.1), calls=%async_computation.1 | async-start | bytes 557056 | tf_op jit(solution)/shard_map/all_to_all | solution.py:320
  87.3 0.8 slice_bitcast_fusion.q_ref
  88.1 0.5 slice.7
  89.2 8.6 %all-to-all-done.1.pieces_ref = bf16[8,136,128]{2,1,0:T(8,128)(2,1)S(1)} async-done(((bf16[8,136,128]{2,1,0:T(8,128)(2,1)}), bf16[8,136,128]{2,1,0:T(8,128)(2,1)S(1)}, u32[]{:S(2)}, u32[]{:S(2)}) %all-to-all-start.1) | async-done | bytes 278560 | tf_op jit(solution)/shard_map/all_to_all | solution.py:320
  97.8 1.3 %finish.1 = bf16[8,4,128]{2,1,0:T(4,128)(2,1)} custom-call(bf16[8,136,128]{2,1,0:T(8,128)(2,1)S(1)} %all-to-all-done.1.pieces_ref, bf16[144,128]{1,0:T(8,128)(2,1)S(1)} %slice_bitcast_fusion.q_ref, bf16[64,512]{1,0:T(8,128)(2,1)S(1)} %copy-done.4, bf16[64,64]{1,0:T(8,128)(2,1)S(1)} %copy-done.6, s32[32,64]{1,0:T(8,128)S(1)} %bitcast.7, ...), custom_call_target="tpu_custom_call" | custom-call | tf_op jit(solution)/shard_map/finish/pallas_call | solution.py:252
  (28 shorter events, 0.1 us)
Async XLA Ops:
  0.6 86.6 %copy-start = (s32[64,64]{1,0:T(8,128)S(1)}, s32[64,64]{1,0:T(8,128)}, u32[]{:S(2)}) copy-start(s32[64,64]{1,0:T(8,128)} %param.16) | copy-start | bytes 49156
  1.3 0.7 copy-start.8
  2.0 1.0 %copy-start.1 = (bf16[512,512]{1,0:T(8,128)(2,1)S(1)}, bf16[512,512]{1,0:T(8,128)(2,1)}, u32[]{:S(2)}) copy-start(bf16[512,512]{1,0:T(8,128)(2,1)} %lat_ref.3) | copy-start | bytes 1572868
  3.0 0.8 copy-start.3
  3.8 18.4 %copy-start.5 = (bf16[8,4,512]{2,1,0:T(4,128)(2,1)S(1)}, bf16[8,4,512]{2,1,0:T(4,128)(2,1)}, u32[]{:S(2)}) copy-start(bf16[8,4,512]{2,1,0:T(4,128)(2,1)} %lat_ref.2) | copy-start | bytes 98308
  3.8 18.4 %copy-start.7 = (bf16[8,64,4]{1,2,0:T(4,128)(2,1)S(1)}, bf16[8,64,4]{1,2,0:T(4,128)(2,1)}, u32[]{:S(2)}) copy-start(bf16[8,64,4]{1,2,0:T(4,128)(2,1)} %param.11) | copy-start | bytes 12292
  4.4 16.3 %collective-permute-start = (bf16[584,512]{1,0:T(8,128)(2,1)S(1)}, bf16[584,512]{1,0:T(8,128)(2,1)S(1)}, u32[]{:S(2)}, u32[]{:S(2)}) collective-permute-start(bf16[584,512]{1,0:T(8,128)(2,1)S(1)} %pack_cache.1.refs_1_), channel_id=1, source_target_pairs={{0,2},{1,7},{2,4},{3,1},{4,6},{5,3},{6,0},{7,5},{8,10},{9,15},{10,... | collective-permute-start | bytes 1794056 | tf_op jit(solution)/shard_map/ppermute | solution.py:271
  6.0 26.0 %collective-permute-start.1 = (bf16[584,512]{1,0:T(8,128)(2,1)S(1)}, bf16[584,512]{1,0:T(8,128)(2,1)S(1)}, u32[]{:S(2)}, u32[]{:S(2)}) collective-permute-start(bf16[584,512]{1,0:T(8,128)(2,1)S(1)} %pack_cache.1.refs_1_), channel_id=1, source_target_pairs={{0,6},{1,3},{2,0},{3,5},{4,2},{5,7},{6,4},{7,1},{8,14},{9,11},{10,... | collective-permute-start | bytes 1794056 | tf_op jit(solution)/shard_map/ppermute | solution.py:271
  20.8 11.4 %collective-permute-start.2 = (bf16[584,512]{1,0:T(8,128)(2,1)S(1)}, bf16[584,512]{1,0:T(8,128)(2,1)S(1)}, u32[]{:S(2)}, u32[]{:S(2)}) collective-permute-start(bf16[584,512]{1,0:T(8,128)(2,1)S(1)} %collective-permute-done.refs_2_), channel_id=1, source_target_pairs={{0,2},{1,7},{2,4},{3,1},{4,6},{5,3},{6,0},{7,5},{8,10},{9,15},{10,... | collective-permute-start | bytes 1794056 | tf_op jit(solution)/shard_map/ppermute | solution.py:271
  23.0 20.9 %all-to-all-start = ((bf16[8,144,128]{2,1,0:T(8,128)(2,1)}), bf16[8,144,128]{2,1,0:T(8,128)(2,1)S(1)}, u32[]{:S(2)}, u32[]{:S(2)}) async-start(bf16[8,144,128]{2,1,0:T(8,128)(2,1)} %pack_query.1), calls=%async_computation | async-start | bytes 589824 | tf_op jit(solution)/shard_map/all_to_all | solution.py:303
  31.5 13.7 %collective-permute-start.3 = (bf16[584,512]{1,0:T(8,128)(2,1)S(1)}, bf16[584,512]{1,0:T(8,128)(2,1)S(1)}, u32[]{:S(2)}, u32[]{:S(2)}) collective-permute-start(bf16[584,512]{1,0:T(8,128)(2,1)S(1)} %pack_cache.1.refs_1_), channel_id=1, source_target_pairs={{0,1},{1,0},{2,3},{3,2},{4,5},{5,4},{6,7},{7,6},{8,9},{9,8},{10,11... | collective-permute-start | bytes 1794056 | tf_op jit(solution)/shard_map/ppermute | solution.py:280
  31.5 24.0 %collective-permute-start.4 = (bf16[584,512]{1,0:T(8,128)(2,1)S(1)}, bf16[584,512]{1,0:T(8,128)(2,1)}, u32[]{:S(2)}, u32[]{:S(2)}) collective-permute-start(bf16[584,512]{1,0:T(8,128)(2,1)S(1)} %collective-permute-done.refs_2_), channel_id=1, source_target_pairs={{0,1},{1,0},{2,3},{3,2},{4,5},{5,4},{6,7},{7,6},{8,9},{9,8},{10,11... | collective-permute-start | bytes 1794056 | tf_op jit(solution)/shard_map/ppermute | solution.py:280
  32.0 23.5 %collective-permute-start.5 = (bf16[584,512]{1,0:T(8,128)(2,1)S(1)}, bf16[584,512]{1,0:T(8,128)(2,1)}, u32[]{:S(2)}, u32[]{:S(2)}) collective-permute-start(bf16[584,512]{1,0:T(8,128)(2,1)S(1)} %collective-permute-done.1.refs_3_), channel_id=1, source_target_pairs={{0,1},{1,0},{2,3},{3,2},{4,5},{5,4},{6,7},{7,6},{8,9},{9,8},{10,11... | collective-permute-start | bytes 1794056 | tf_op jit(solution)/shard_map/ppermute | solution.py:280
  32.1 23.4 %collective-permute-start.6 = (bf16[584,512]{1,0:T(8,128)(2,1)S(1)}, bf16[584,512]{1,0:T(8,128)(2,1)}, u32[]{:S(2)}, u32[]{:S(2)}) collective-permute-start(bf16[584,512]{1,0:T(8,128)(2,1)S(1)} %collective-permute-done.2.refs_4_), channel_id=1, source_target_pairs={{0,1},{1,0},{2,3},{3,2},{4,5},{5,4},{6,7},{7,6},{8,9},{9,8},{10,11... | collective-permute-start | bytes 1794056 | tf_op jit(solution)/shard_map/ppermute | solution.py:280
  44.0 9.1 %collective-permute-start.7 = (bf16[8,144,128]{2,1,0:T(8,128)(2,1)S(1)}, bf16[8,144,128]{2,1,0:T(8,128)(2,1)S(1)}, u32[]{:S(2)}, u32[]{:S(2)}) collective-permute-start(bf16[8,144,128]{2,1,0:T(8,128)(2,1)S(1)} %all-to-all-done.refs_0_), channel_id=1, source_target_pairs={{0,16},{8,24},{16,0},{24,8},{1,17},{9,25},{17,1},{25,9},{2,18},{10... | collective-permute-start | bytes 884744 | tf_op jit(solution)/shard_map/ppermute | solution.py:276
  45.2 18.2 %collective-permute-start.11 = (bf16[8,144,128]{2,1,0:T(8,128)(2,1)S(1)}, bf16[8,144,128]{2,1,0:T(8,128)(2,1)S(1)}, u32[]{:S(2)}, u32[]{:S(2)}) collective-permute-start(bf16[8,144,128]{2,1,0:T(8,128)(2,1)S(1)} %all-to-all-done.refs_0_), channel_id=1, source_target_pairs={{0,24},{1,9},{8,0},{9,17},{16,8},{17,25},{24,16},{25,1},{2,26},{3,... | collective-permute-start | bytes 884744 | tf_op jit(solution)/shard_map/ppermute | solution.py:271
  53.1 16.4 %collective-permute-start.9 = (bf16[8,144,128]{2,1,0:T(8,128)(2,1)S(1)}, bf16[8,144,128]{2,1,0:T(8,128)(2,1)S(1)}, u32[]{:S(2)}, u32[]{:S(2)}) collective-permute-start(bf16[8,144,128]{2,1,0:T(8,128)(2,1)S(1)} %all-to-all-done.refs_0_), channel_id=1, source_target_pairs={{0,8},{1,25},{8,16},{9,1},{16,24},{17,9},{24,0},{25,17},{2,10},{3,... | collective-permute-start | bytes 884744 | tf_op jit(solution)/shard_map/ppermute | solution.py:271
  60.5 21.3 %collective-permute-start.8 = (bf16[8,136,128]{2,1,0:T(8,128)(2,1)S(1)}, bf16[8,136,128]{2,1,0:T(8,128)(2,1)S(1)}, u32[]{:S(2)}, u32[]{:S(2)}) collective-permute-start(bf16[8,136,128]{2,1,0:T(8,128)(2,1)S(1)} %get-tuple-element.8), channel_id=1, source_target_pairs={{0,16},{8,24},{16,0},{24,8},{1,17},{9,25},{17,1},{25,9},{2,18},{10... | collective-permute-start | bytes 835592 | tf_op jit(solution)/shard_map/ppermute | solution.py:276
  68.8 13.0 %collective-permute-start.12 = (bf16[8,136,128]{2,1,0:T(8,128)(2,1)S(1)}, bf16[8,136,128]{2,1,0:T(8,128)(2,1)S(1)}, u32[]{:S(2)}, u32[]{:S(2)}) collective-permute-start(bf16[8,136,128]{2,1,0:T(8,128)(2,1)S(1)} %get-tuple-element.10), channel_id=1, source_target_pairs={{0,8},{1,25},{8,16},{9,1},{16,24},{17,9},{24,0},{25,17},{2,10},{3,... | collective-permute-start | bytes 835592 | tf_op jit(solution)/shard_map/ppermute | solution.py:271
  74.9 7.8 %collective-permute-start.10 = (bf16[8,136,128]{2,1,0:T(8,128)(2,1)S(1)}, bf16[8,136,128]{2,1,0:T(8,128)(2,1)S(1)}, u32[]{:S(2)}, u32[]{:S(2)}) collective-permute-start(bf16[8,136,128]{2,1,0:T(8,128)(2,1)S(1)} %get-tuple-element.9), channel_id=1, source_target_pairs={{0,24},{1,9},{8,0},{9,17},{16,8},{17,25},{24,16},{25,1},{2,26},{3,... | collective-permute-start | bytes 835592 | tf_op jit(solution)/shard_map/ppermute | solution.py:271
  83.7 14.1 %copy-start.2 = (bf16[4,512,128]{2,1,0:T(8,128)(2,1)S(1)}, bf16[4,512,128]{2,1,0:T(8,128)(2,1)}, u32[]{:S(2)}) copy-start(bf16[4,512,128]{2,1,0:T(8,128)(2,1)} %w_ref.1) | copy-start | bytes 1572868
  83.7 14.1 %all-to-all-start.1 = ((bf16[8,136,128]{2,1,0:T(8,128)(2,1)}), bf16[8,136,128]{2,1,0:T(8,128)(2,1)S(1)}, u32[]{:S(2)}, u32[]{:S(2)}) async-start(bf16[8,136,128]{2,1,0:T(8,128)(2,1)} %merge.1), calls=%async_computation.1 | async-start | bytes 557056 | tf_op jit(solution)/shard_map/all_to_all | solution.py:320
  87.3 10.6 %copy-start.4 = (bf16[64,512]{1,0:T(8,128)(2,1)S(1)}, bf16[64,512]{1,0:T(8,128)(2,1)}, u32[]{:S(2)}) copy-start(bf16[64,512]{1,0:T(8,128)(2,1)} %d_lat_ref.1) | copy-start | bytes 196612
  88.1 9.8 %copy-start.6 = (bf16[64,64]{1,0:T(8,128)(2,1)S(1)}, bf16[64,64]{1,0:T(8,128)(2,1)}, u32[]{:S(2)}) copy-start(bf16[64,64]{1,0:T(8,128)(2,1)} %d_rope_ref.1) | copy-start | bytes 24580
where the time goes:
time: 101 us; the launch traced here: 100 us
  waiting for transfers between devices  41.8 us (41%)
  starting transfers between devices  26.5 us (26%)
  Pallas kernels  25 us (25%)
  local copies, waits for them, and re-layouts  3.86 us (4%)
  between operations  3.18 us (3%)
    pallas_call x4, Pallas kernels, attend(): pl.pallas_call(functools.partial(attend_kernel, len(queries), n), out_sha...  21.3 us
    ppermute x7, waiting for transfers between devices, shift(): lax.ppermute(value, (axis, 'core'), both_ways(lax.axis_size(axis), step))  13.9 us
    all_to_all x1, waiting for transfers between devices, shards(): near = lax.all_to_all(packed, 'z', 0, 0, tiled=True)  11.4 us
    ppermute x7, starting transfers between devices, shift(): lax.ppermute(value, (axis, 'core'), both_ways(lax.axis_size(axis), step))  9.34 us
    all_to_all x1, waiting for transfers between devices, shards(): pieces = lax.all_to_all(pieces, 'z', 0, 0, tiled=True)  8.58 us
    all_to_all x1, starting transfers between devices, shards(): near = lax.all_to_all(packed, 'z', 0, 0, tiled=True)  8.47 us
    ppermute x2, waiting for transfers between devices, across(): return lax.ppermute(value, axis, [(i, (i + n // 2) % n) for i in range(n)])  7.86 us
    ppermute x2, starting transfers between devices, across(): return lax.ppermute(value, axis, [(i, (i + n // 2) % n) for i in range(n)])  4.09 us
  transfers between devices with their start and end apart: 15, of which 5 were waited for; matrix products, arithmetic and copies ran while one was open for 1% of the time, Pallas kernels for 22%

commit v1 on v0

--- a/solution.py
+++ b/solution.py
@@ -38,18 +38,20 @@
     return high, middle, low
 
 
-def attend_kernel(n_queries, n_chunks, *refs):
+def attend_kernel(n_queries, n_chunks, counted, *refs):
     q_refs, chunks = refs[:n_queries], refs[n_queries : n_queries + n_chunks]
-    out_ref, count_ref, query, query_rope, scores = refs[n_queries + n_chunks :]
+    out_ref = refs[n_queries + n_chunks]
+    query, query_rope, scores = refs[-3:]
     rows = LATENT
     lane = lax.broadcasted_iota(jnp.int32, (BLOCK, LANES), 1)
     query_rope[...] = jnp.where(lane == ROPE, 1.0, 0.0).astype(jnp.bfloat16)
     own_lane = lax.broadcasted_iota(jnp.int32, (ROWS, LANES), 1)
     own_row = lax.broadcasted_iota(jnp.int32, (ROWS, LANES), 0)
-    count = jnp.zeros((EXTRA, LANES), jnp.float32)
-    for c in range(n_chunks):
-        count = count + chunks[c][rows + ROPE :, :LANES].astype(jnp.float32)
-    count_ref[...] = count
+    if counted:
+        count = jnp.zeros((EXTRA, LANES), jnp.float32)
+        for c in range(n_chunks):
+            count = count + chunks[c][rows + ROPE :, :LANES].astype(jnp.float32)
+        refs[n_queries + n_chunks + 1][...] = count
     owners = [q_ref.at[i] for q_ref in q_refs for i in range(q_ref.shape[0])]
     for i in range(OWNERS):
         for j in range(4):
@@ -94,17 +96,17 @@
     return jnp.concatenate(parts + [pad], axis=0).astype(jnp.bfloat16)
 
 
-def attend(queries, chunks):
+def attend(queries, chunks, counted=False):
     vmem = pl.BlockSpec(memory_space=pltpu.VMEM)
     n = len(chunks)
     return pl.pallas_call(
-        functools.partial(attend_kernel, len(queries), n),
-        out_shape=(
+        functools.partial(attend_kernel, len(queries), n, counted),
+        out_shape=[
             jax.ShapeDtypeStruct((OWNERS, O_ROWS, LANES), jnp.bfloat16),
             jax.ShapeDtypeStruct((EXTRA, LANES), jnp.float32),
-        ),
+        ][: 2 if counted else 1],
         in_specs=[vmem] * (len(queries) + n),
-        out_specs=(vmem, vmem),
+        out_specs=[vmem] * (2 if counted else 1),
         scratch_shapes=[
             pltpu.VMEM((BLOCK, LATENT), jnp.bfloat16),
             pltpu.VMEM((BLOCK, LANES), jnp.bfloat16),
@@ -118,11 +120,16 @@
     )(*queries, *chunks)
 
 
-def merge_kernel(*refs):
-    pieces, out_ref = refs[:-1], refs[-1]
+def merge_kernel(n_pieces, *refs):
+    pieces, outs = refs[:n_pieces], refs[n_pieces:]
+    place = lax.axis_index("z")
+    n = pieces[0].shape[0]
     own_lane = lax.broadcasted_iota(jnp.int32, (ROWS, LANES), 1)
     diagonal = own_lane == lax.broadcasted_iota(jnp.int32, (ROWS, LANES), 0)
-    for i in range(out_ref.shape[0]):
+    owners = [lax.rem(place - 2 * (i // 2) + n, n) for i in range(n)]
+    owners = [z + (i % 2) * (1 - 2 * lax.rem(z, 2)) for i, z in enumerate(owners)]
+    blocks = [outs[0].at[z] for z in owners]
+    for i, out in enumerate(blocks):
         lses = []
         for piece in pieces:
             parts = piece[i, 4 * ROWS :, :].astype(jnp.float32)
@@ -130,7 +137,7 @@
         peak = functools.reduce(jnp.maximum, lses)
         shares = [jnp.exp2(lse - peak) for lse in lses]
         total = sum(shares[1:], shares[0])
-        out_ref[i, 4 * ROWS :, :] = lines_of(peak + jnp.log2(total))
+        out[4 * ROWS :, :] = lines_of(peak + jnp.log2(total))
         shares = [
             jnp.sum(jnp.where(diagonal, share / total, 0.0), axis=1, keepdims=True)
             for share in shares
@@ -138,16 +145,17 @@
         for j in range(4):
             mine = slice(j * ROWS, (j + 1) * ROWS)
             latent = sum(p[i, mine, :].astype(jnp.float32) * s for p, s in zip(pieces, shares))
-            out_ref[i, mine, :] = latent.astype(jnp.bfloat16)
-
-
-def merge(pieces):
+            out[mine, :] = latent.astype(jnp.bfloat16)
+
+
+def merge(pieces, groups):
     vmem = pl.BlockSpec(memory_space=pltpu.VMEM)
-    return pl.pallas_call(
-        merge_kernel,
-        out_shape=jax.ShapeDtypeStruct(pieces[0].shape, pieces[0].dtype),
+    n, rest = pieces[0].shape[0], pieces[0].shape[1:]
+    return pl.pallas_call(
+        functools.partial(merge_kernel, len(pieces)),
+        out_shape=[jax.ShapeDtypeStruct((n // groups, *rest), jnp.bfloat16)] * groups,
         in_specs=[vmem] * len(pieces),
-        out_specs=vmem,
+        out_specs=[vmem] * groups,
         compiler_params=pltpu.CompilerParams(vmem_limit_bytes=8 * 2**20),
         name="merge",
     )(*pieces)
@@ -181,35 +189,44 @@
     )(q_latent, q_rope)
 
 
-def pack_cache_kernel(valid_ref, accepted_ref, lat_ref, rope_ref, out_ref):
+def pack_cache_kernel(valid_ref, accepted_ref, lat, rope, out_ref, sems):
+    copies = [
+        pltpu.make_async_copy(lat, out_ref.at[:LATENT], sems.at[0]),
+        pltpu.make_async_copy(rope, out_ref.at[LATENT : LATENT + ROPE], sems.at[1]),
+    ]
+    for copy in copies:
+        copy.start()
     limit = valid_ref[0] - lax.axis_index(SEQ + BLK) * LATENT
     count = sum(accepted_ref[i] for i in range(accepted_ref.shape[0]))
-    out_ref[:LATENT, :] = lat_ref[...]
-    out_ref[LATENT : LATENT + ROPE, :] = rope_ref[...]
     lane = lax.broadcasted_iota(jnp.int32, (EXTRA, LATENT), 1)
     row = lax.broadcasted_iota(jnp.int32, (EXTRA, LATENT), 0)
     dead = jnp.where((row == 0) & (lane >= limit), NEG, 0.0)
     extra = jnp.where(row == 1, count.astype(jnp.float32), dead)
     out_ref[LATENT + ROPE :, :] = extra.astype(jnp.bfloat16)
+    copies[0].wait()
+    copies[1].wait()
 
 
 def pack_cache(valid_length, accepted, cache_latent, cache_rope):
-    vmem = pl.BlockSpec(memory_space=pltpu.VMEM)
-    smem = pl.BlockSpec(memory_space=pltpu.SMEM)
     return pl.pallas_call(
         pack_cache_kernel,
         out_shape=jax.ShapeDtypeStruct((LATENT + ROPE + EXTRA, LATENT), jnp.bfloat16),
-        in_specs=[smem, smem, vmem, vmem],
-        out_specs=vmem,
-        compiler_params=pltpu.CompilerParams(vmem_limit_bytes=8 * 2**20),
+        in_specs=[pl.BlockSpec(memory_space=pltpu.SMEM)] * 2
+        + [pl.BlockSpec(memory_space=pltpu.HBM)] * 2,
+        out_specs=pl.BlockSpec(memory_space=pltpu.VMEM),
+        scratch_shapes=[pltpu.SemaphoreType.DMA((2,))],
+        compiler_params=pltpu.CompilerParams(vmem_limit_bytes=60 * 1024 * 2**10 - 660 * 2**10),
         name="pack_cache",
     )(valid_length.reshape(1), accepted, cache_latent, cache_rope)
 
 
 def finish_kernel(tokens, heads, pieces_ref, q_ref, d_lat_ref, d_rope_ref, tree_ref, w_ref, out_ref):
-    n = pieces_ref.shape[0]
-    parts = pieces_ref[:, 4 * ROWS :, :].astype(jnp.float32)
-    lse = parts[:, 0, :] + parts[:, 1, :] + parts[:, 2, :]
+    pieces = [pieces_ref.at[i] for i in range(pieces_ref.shape[0])]
+    lses = []
+    for piece in pieces:
+        parts = piece[4 * ROWS :, :].astype(jnp.float32)
+        lses.append(parts[0:1, :] + parts[1:2, :] + parts[2:3, :])
+    q_ref = q_ref.at[0]
     query = jnp.concatenate([q_ref[j * ROWS : (j + 1) * ROWS, :] for j in range(4)], axis=1)
     both = q_ref[4 * ROWS :, :]
     query_rope = jnp.concatenate([both[:, :ROPE], both[:, ROPE:]], axis=0)
@@ -224,17 +241,15 @@
     def to_rows(line):
         return jnp.sum(jnp.where(diagonal, line, 0.0), axis=1, keepdims=True)
 
-    cache_peak = to_rows(jnp.max(lse, axis=0, keepdims=True))
+    cache_peak = to_rows(functools.reduce(jnp.maximum, lses))
     peak = jnp.maximum(cache_peak, draft_peak)
     weight = jnp.exp2(score - peak)
     total = jnp.sum(weight, axis=1, keepdims=True)
     latent = dot(weight.astype(jnp.bfloat16), draft)
-    for i in range(n):
-        share = jnp.exp2(to_rows(lse[i : i + 1, :]) - peak)
+    for piece, lse in zip(pieces, lses):
+        share = jnp.exp2(to_rows(lse) - peak)
         total = total + share
-        piece = jnp.concatenate(
-            [pieces_ref[i, j * ROWS : (j + 1) * ROWS, :] for j in range(4)], axis=1
-        )
+        piece = jnp.concatenate([piece[j * ROWS : (j + 1) * ROWS, :] for j in range(4)], axis=1)
         latent = latent + share * piece.astype(jnp.float32)
     latent = latent / total
     high = latent.astype(jnp.bfloat16)
@@ -274,6 +289,15 @@
 def across(value, axis):
     n = lax.axis_size(axis)
     return lax.ppermute(value, axis, [(i, (i + n // 2) % n) for i in range(n)])
+
+
+def pair(value, axis):
+    return lax.ppermute(value, axis, [(i, i ^ 1) for i in range(lax.axis_size(axis))])
+
+
+def rotate(value, axis, step):
+    n = lax.axis_size(axis)
+    return lax.ppermute(value, axis, [(i, (i + step) % n) for i in range(n)])
 
 
 def other_core(value):
@@ -295,12 +319,16 @@
     tokens, heads = q_latent.shape[:2]
     nz = lax.axis_size("z")
 
-    packed = pack_query(q_latent, q_rope.transpose(0, 2, 1), nz)
+    packed = pack_query(q_latent, q_rope.transpose(0, 2, 1), 1)
     own = pack_cache(valid_length, accepted, cache_latent, cache_rope)
     ahead = shift(own, "x", 1)
     behind = shift(own, "x", -1)
     far = shift(ahead, "x", 1)
-    near = lax.all_to_all(packed, "z", 0, 0, tiled=True)
+    near = jnp.concatenate([packed, pair(packed, "z")], axis=0)
+    turned = [near]
+    for step in range(2, nz, 2):
+        turned.append(rotate(near, "z", step))
+    near = jnp.concatenate(turned, axis=0)
     q_far = across(near, "y")
     q_ahead = shift(near, "y", 1)
     q_behind = shift(near, "y", -1)
@@ -309,18 +337,18 @@
     for chunk in mine:
         chunks.append(other_core(chunk))
 
-    part_far, counts = attend((q_far,), chunks)
-    part_ahead, _ = attend((q_ahead,), chunks)
-    part_behind, _ = attend((q_behind,), chunks)
-    part_near, _ = attend((near,), chunks)
+    part_far, counts = attend((q_far,), chunks, counted=True)
+    (part_ahead,) = attend((q_ahead,), chunks)
+    (part_behind,) = attend((q_behind,), chunks)
+    (part_near,) = attend((near,), chunks)
     from_far = across(part_far, "y")
     from_ahead = shift(part_ahead, "y", -1)
     from_behind = shift(part_behind, "y", 1)
-    pieces = merge((part_near, from_far, from_ahead, from_behind))
+    (pieces,) = merge((part_near, from_far, from_ahead, from_behind), 1)
     pieces = lax.all_to_all(pieces, "z", 0, 0, tiled=True)
     tree = lax.dynamic_slice_in_dim(ancestors, lax.axis_index(BLK) * tokens, tokens, 0)
     tree = jnp.repeat(tree, heads, axis=0)
-    attended = finish(pieces, packed[0], draft_latent, draft_rope, tree, w_value, tokens, heads)
+    attended = finish(pieces, packed, draft_latent, draft_rope, tree, w_value, tokens, heads)
     return (attended, counts[1, 0].astype(jnp.int32))
 
 

time: 101 us -> 108 us (1.069)
  the two profiles are of different devices: /device:TPU:24 before, /device:TPU:2 now
where the time goes in v1:
time: 108 us; the launch traced here: 107 us
  waiting for transfers between devices  42.5 us (39%)
  starting transfers between devices  41.9 us (39%)
  Pallas kernels  19.3 us (18%)
  between operations  3.24 us (3%)
    ppermute x7, waiting for transfers between devices, shift(): lax.ppermute(value, (axis, 'core'), both_ways(lax.axis_size(axis), step))  20.2 us
    pallas_call x4, Pallas kernels, attend(): pl.pallas_call(functools.partial(attend_kernel, len(queries), n, counted)...  14.2 us
    all_to_all x1, starting transfers between devices, shards(): pieces = lax.all_to_all(pieces, 'z', 0, 0, tiled=True)  13.4 us
    ppermute x3, starting transfers between devices, rotate(): return lax.ppermute(value, axis, [(i, (i + step) % n) for i in range(n)])  12.6 us
    all_to_all x1, waiting for transfers between devices, shards(): pieces = lax.all_to_all(pieces, 'z', 0, 0, tiled=True)  9.46 us
    ppermute x7, starting transfers between devices, shift(): lax.ppermute(value, (axis, 'core'), both_ways(lax.axis_size(axis), step))  9.08 us
    ppermute x3, waiting for transfers between devices, rotate(): return lax.ppermute(value, axis, [(i, (i + step) % n) for i in range(n)])  6.27 us
    ppermute x2, waiting for transfers between devices, across(): return lax.ppermute(value, axis, [(i, (i + n // 2) % n) for i in range(n)])  4.47 us
  transfers between devices with their start and end apart: 18, of which 9 were waited for; matrix products, arithmetic and copies ran while one was open for 1% of the time, Pallas kernels for 13%

profile of v1, /device:TPU:2, one launch (start us, length us, event | category | flops | bytes accessed | tf_op | source)
XLA Modules:
  0.0 107.5 jit_solution(9022364658089245814)
XLA Ops:
  1.3 2.7 %pack_cache.1.refs_1_ = bf16[584,512]{1,0:T(8,128)(2,1)} custom-call(s32[1]{0:T(128)} %bitcast.4.valid_ref, s32[8]{0:T(128)} %accepted_ref.1, bf16[512,512]{1,0:T(8,128)(2,1)} %lat.1, bf16[64,512]{1,0:T(8,128)(2,1)} %rope.1), custom_call_target="tpu_custom_call" | custom-call | tf_op jit(solution)/shard_map/pack_cache/pallas_call | solution.py:211
  4.0 1.6 %collective-permute-start.4 = (bf16[584,512]{1,0:T(8,128)(2,1)}, bf16[584,512]{1,0:T(8,128)(2,1)S(1)}, u32[]{:S(2)}, u32[]{:S(2)}) collective-permute-start(bf16[584,512]{1,0:T(8,128)(2,1)} %pack_cache.1.refs_1_), channel_id=1, source_target_pairs={{0,2},{1,7},{2,4},{3,1},{4,6},{5,3},{6,0},{7,5},{8,10},{9,15},{10,... | collective-permute-start | bytes 1794056 | tf_op jit(solution)/shard_map/ppermute | solution.py:286
  5.6 0.8 collective-permute-start.5
  6.5 14.4 %collective-permute-done.4.refs_2_ = bf16[584,512]{1,0:T(8,128)(2,1)S(1)} collective-permute-done((bf16[584,512]{1,0:T(8,128)(2,1)}, bf16[584,512]{1,0:T(8,128)(2,1)S(1)}, u32[]{:S(2)}, u32[]{:S(2)}) %collective-permute-start.4) | collective-permute-done | bytes 598048 | tf_op jit(solution)/shard_map/ppermute | solution.py:286
  20.9 0.4 collective-permute-start.6
  21.4 2.0 %collective-permute-start = (bf16[1,144,128]{2,1,0:T(8,128)(2,1)S(1)}, bf16[1,144,128]{2,1,0:T(8,128)(2,1)S(1)}, u32[]{:S(2)}, u32[]{:S(2)}) collective-permute-start(bf16[1,144,128]{2,1,0:T(8,128)(2,1)S(1)} %pack_query.1.q_ref), channel_id=1, source_target_pairs={{0,32},{32,0},{64,96},{96,64},{128,160},{160,128},{192,224},{224,1... | collective-permute-start | bytes 110600 | tf_op jit(solution)/shard_map/ppermute | solution.py:295
  23.4 2.1 %collective-permute-done = bf16[1,144,128]{2,1,0:T(8,128)(2,1)S(1)} collective-permute-done((bf16[1,144,128]{2,1,0:T(8,128)(2,1)S(1)}, bf16[1,144,128]{2,1,0:T(8,128)(2,1)S(1)}, u32[]{:S(2)}, u32[]{:S(2)}) %collective-permute-start) | collective-permute-done | bytes 36896 | tf_op jit(solution)/shard_map/ppermute | solution.py:295
  25.5 3.3 %collective-permute-start.1 = (bf16[2,144,128]{2,1,0:T(8,128)(2,1)S(1)}, bf16[2,144,128]{2,1,0:T(8,128)(2,1)S(1)}, u32[]{:S(2)}, u32[]{:S(2)}) collective-permute-start(bf16[2,144,128]{2,1,0:T(8,128)(2,1)S(1)} %pad_maximum_fusion), channel_id=1, source_target_pairs={{0,64},{32,96},{64,128},{96,160},{128,192},{160,224},{192,0},{224,... | collective-permute-start | bytes 221192 | tf_op jit(solution)/shard_map/ppermute | solution.py:300
  28.9 5.3 %collective-permute-start.2 = (bf16[2,144,128]{2,1,0:T(8,128)(2,1)S(1)}, bf16[2,144,128]{2,1,0:T(8,128)(2,1)S(1)}, u32[]{:S(2)}, u32[]{:S(2)}) collective-permute-start(bf16[2,144,128]{2,1,0:T(8,128)(2,1)S(1)} %pad_maximum_fusion), channel_id=1, source_target_pairs={{0,128},{32,160},{64,192},{96,224},{128,0},{160,32},{192,64},{224,... | collective-permute-start | bytes 221192 | tf_op jit(solution)/shard_map/ppermute | solution.py:300
  34.2 0.5 collective-permute-done.1
  34.7 0.5 collective-permute-start.9
  35.3 3.8 %collective-permute-done.2 = bf16[2,144,128]{2,1,0:T(8,128)(2,1)S(1)} collective-permute-done((bf16[2,144,128]{2,1,0:T(8,128)(2,1)S(1)}, bf16[2,144,128]{2,1,0:T(8,128)(2,1)S(1)}, u32[]{:S(2)}, u32[]{:S(2)}) %collective-permute-start.2) | collective-permute-done | bytes 73760 | tf_op jit(solution)/shard_map/ppermute | solution.py:300
  39.1 4.0 %collective-permute-start.3 = (bf16[2,144,128]{2,1,0:T(8,128)(2,1)S(1)}, bf16[2,144,128]{2,1,0:T(8,128)(2,1)S(1)}, u32[]{:S(2)}, u32[]{:S(2)}) collective-permute-start(bf16[2,144,128]{2,1,0:T(8,128)(2,1)S(1)} %pad_maximum_fusion), channel_id=1, source_target_pairs={{0,192},{32,224},{64,0},{96,32},{128,64},{160,96},{192,128},{224,1... | collective-permute-start | bytes 221192 | tf_op jit(solution)/shard_map/ppermute | solution.py:300
  43.1 2.0 %collective-permute-done.3 = bf16[2,144,128]{2,1,0:T(8,128)(2,1)S(1)} collective-permute-done((bf16[2,144,128]{2,1,0:T(8,128)(2,1)S(1)}, bf16[2,144,128]{2,1,0:T(8,128)(2,1)S(1)}, u32[]{:S(2)}, u32[]{:S(2)}) %collective-permute-start.3) | collective-permute-done | bytes 73760 | tf_op jit(solution)/shard_map/ppermute | solution.py:300
  45.1 3.1 %collective-permute-start.15 = (bf16[8,144,128]{2,1,0:T(8,128)(2,1)S(1)}, bf16[8,144,128]{2,1,0:T(8,128)(2,1)S(1)}, u32[]{:S(2)}, u32[]{:S(2)}) collective-permute-start(bf16[8,144,128]{2,1,0:T(8,128)(2,1)S(1)} %constant_dynamic-update-slice_fusion.refs_0_), channel_id=1, source_target_pairs={{0,24},{1,9},{8,0},{9,17},{16,8},{17,25},{24,16},{25,1},{2,26},{3,... | collective-permute-start | bytes 884744 | tf_op jit(solution)/shard_map/ppermute | solution.py:286
  48.2 4.2 %collective-permute-done.15.refs_0_ = bf16[8,144,128]{2,1,0:T(8,128)(2,1)S(1)} collective-permute-done((bf16[8,144,128]{2,1,0:T(8,128)(2,1)S(1)}, bf16[8,144,128]{2,1,0:T(8,128)(2,1)S(1)}, u32[]{:S(2)}, u32[]{:S(2)}) %collective-permute-start.15) | collective-permute-done | bytes 294944 | tf_op jit(solution)/shard_map/ppermute | solution.py:286
  52.4 1.0 collective-permute-start.13
  53.5 4.1 %collective-permute-start.11 = (bf16[8,144,128]{2,1,0:T(8,128)(2,1)S(1)}, bf16[8,144,128]{2,1,0:T(8,128)(2,1)S(1)}, u32[]{:S(2)}, u32[]{:S(2)}) collective-permute-start(bf16[8,144,128]{2,1,0:T(8,128)(2,1)S(1)} %constant_dynamic-update-slice_fusion.refs_0_), channel_id=1, source_target_pairs={{0,16},{8,24},{16,0},{24,8},{1,17},{9,25},{17,1},{25,9},{2,18},{10... | collective-permute-start | bytes 884744 | tf_op jit(solution)/shard_map/ppermute | solution.py:291
  57.6 3.5 %attend.7 = bf16[8,136,128]{2,1,0:T(8,128)(2,1)S(1)} custom-call(bf16[8,144,128]{2,1,0:T(8,128)(2,1)S(1)} %collective-permute-done.15.refs_0_, bf16[584,512]{1,0:T(8,128)(2,1)S(1)} %copy-done.1, bf16[584,512]{1,0:T(8,128)(2,1)S(1)} %collective-permute-done.4.refs_2_, bf16[584,512]{1,0:T(8,128)(2,1)S(1)} %collective-permute-done.5.refs_3_, ...), custom_call_target="tpu_custom_call" | custom-call | flops 2684354560 | bytes 1048576 | tf_op jit(solution)/shard_map/attend/pallas_call | solution.py:102
  61.2 0.3 collective-permute-start.16
  61.4 1.5 %collective-permute-done.13.refs_0_ = bf16[8,144,128]{2,1,0:T(8,128)(2,1)S(1)} collective-permute-done((bf16[8,144,128]{2,1,0:T(8,128)(2,1)S(1)}, bf16[8,144,128]{2,1,0:T(8,128)(2,1)S(1)}, u32[]{:S(2)}, u32[]{:S(2)}) %collective-permute-start.13) | collective-permute-done | bytes 294944 | tf_op jit(solution)/shard_map/ppermute | solution.py:286
  62.9 3.5 %attend.6 = bf16[8,136,128]{2,1,0:T(8,128)(2,1)S(1)} custom-call(bf16[8,144,128]{2,1,0:T(8,128)(2,1)S(1)} %collective-permute-done.13.refs_0_, bf16[584,512]{1,0:T(8,128)(2,1)S(1)} %copy-done.1, bf16[584,512]{1,0:T(8,128)(2,1)S(1)} %collective-permute-done.4.refs_2_, bf16[584,512]{1,0:T(8,128)(2,1)S(1)} %collective-permute-done.5.refs_3_, ...), custom_call_target="tpu_custom_call" | custom-call | flops 2684354560 | bytes 1048576 | tf_op jit(solution)/shard_map/attend/pallas_call | solution.py:102
  66.5 1.8 %collective-permute-start.14 = (bf16[8,136,128]{2,1,0:T(8,128)(2,1)S(1)}, bf16[8,136,128]{2,1,0:T(8,128)(2,1)S(1)}, u32[]{:S(2)}, u32[]{:S(2)}) collective-permute-start(bf16[8,136,128]{2,1,0:T(8,128)(2,1)S(1)} %attend.6), channel_id=1, source_target_pairs={{0,24},{1,9},{8,0},{9,17},{16,8},{17,25},{24,16},{25,1},{2,26},{3,... | collective-permute-start | bytes 835592 | tf_op jit(solution)/shard_map/ppermute | solution.py:286
  68.3 3.5 %attend.5 = (bf16[8,136,128]{2,1,0:T(8,128)(2,1)S(1)}, f32[8,128]{1,0:T(8,128)S(1)}) custom-call(bf16[8,144,128]{2,1,0:T(8,128)(2,1)S(1)} %collective-permute-done.11.refs_0_, bf16[584,512]{1,0:T(8,128)(2,1)S(1)} %copy-done.1, bf16[584,512]{1,0:T(8,128)(2,1)S(1)} %collective-permute-done.4.refs_2_, bf16[584,512]{1,0:T(8,128)(2,1)S(1)} %collective-permute-done.5.refs_3_, ...), custom_call_target="tpu_custom_call" | custom-call | flops 2684354560 | bytes 1048576 | tf_op jit(solution)/shard_map/attend/pallas_call | solution.py:102
  71.8 0.1 collective-permute-start.12
  71.9 3.5 %attend.4.refs_0_ = bf16[8,136,128]{2,1,0:T(8,128)(2,1)S(1)} custom-call(bf16[8,144,128]{2,1,0:T(8,128)(2,1)S(1)} %constant_dynamic-update-slice_fusion.refs_0_, bf16[584,512]{1,0:T(8,128)(2,1)S(1)} %copy-done.1, bf16[584,512]{1,0:T(8,128)(2,1)S(1)} %collective-permute-done.4.refs_2_, bf16[584,512]{1,0:T(8,128)(2,1)S(1)} %collective-permute-done.5.refs_3_, ...), custom_call_target="tpu_custom_call" | custom-call | flops 2684354560 | bytes 1048576 | tf_op jit(solution)/shard_map/attend/pallas_call | solution.py:102
  75.5 4.5 %collective-permute-done.12.refs_1_ = bf16[8,136,128]{2,1,0:T(8,128)(2,1)S(1)} collective-permute-done((bf16[8,136,128]{2,1,0:T(8,128)(2,1)S(1)}, bf16[8,136,128]{2,1,0:T(8,128)(2,1)S(1)}, u32[]{:S(2)}, u32[]{:S(2)}) %collective-permute-start.12) | collective-permute-done | bytes 278560 | tf_op jit(solution)/shard_map/ppermute | solution.py:291
  80.0 1.0 merge.1
  81.0 13.4 %all-to-all-start = ((bf16[8,136,128]{2,1,0:T(8,128)(2,1)}), bf16[8,136,128]{2,1,0:T(8,128)(2,1)S(1)}, u32[]{:S(2)}, u32[]{:S(2)}) async-start(bf16[8,136,128]{2,1,0:T(8,128)(2,1)} %merge.1), calls=%async_computation | async-start | bytes 557056 | tf_op jit(solution)/shard_map/all_to_all | solution.py:348
  94.4 0.5 slice.3
  95.6 9.5 %all-to-all-done.pieces_ref = bf16[8,136,128]{2,1,0:T(8,128)(2,1)S(1)} async-done(((bf16[8,136,128]{2,1,0:T(8,128)(2,1)}), bf16[8,136,128]{2,1,0:T(8,128)(2,1)S(1)}, u32[]{:S(2)}, u32[]{:S(2)}) %all-to-all-start) | async-done | bytes 278560 | tf_op jit(solution)/shard_map/all_to_all | solution.py:348
  105.1 1.3 %finish.1 = bf16[8,4,128]{2,1,0:T(4,128)(2,1)} custom-call(bf16[8,136,128]{2,1,0:T(8,128)(2,1)S(1)} %all-to-all-done.pieces_ref, bf16[1,144,128]{2,1,0:T(8,128)(2,1)S(1)} %pack_query.1.q_ref, bf16[64,512]{1,0:T(8,128)(2,1)S(1)} %copy-done.3, bf16[64,64]{1,0:T(8,128)(2,1)S(1)} %copy-done.5, s32[32,64]{1,0:T(8,128)S(1)} %bitcast.5, ...), custom_call_target="tpu_custom_call" | custom-call | tf_op jit(solution)/shard_map/finish/pallas_call | solution.py:267
  (35 shorter events, 0.3 us)
Async XLA Ops:
  0.6 93.7 %copy-start = (s32[64,64]{1,0:T(8,128)S(1)}, s32[64,64]{1,0:T(8,128)}, u32[]{:S(2)}) copy-start(s32[64,64]{1,0:T(8,128)} %param.16) | copy-start | bytes 49156
  1.3 20.0 %copy-start.4 = (bf16[8,4,512]{2,1,0:T(4,128)(2,1)S(1)}, bf16[8,4,512]{2,1,0:T(4,128)(2,1)}, u32[]{:S(2)}) copy-start(bf16[8,4,512]{2,1,0:T(4,128)(2,1)} %lat_ref.1) | copy-start | bytes 98308
  1.3 20.0 %copy-start.6 = (bf16[8,64,4]{1,2,0:T(4,128)(2,1)S(1)}, bf16[8,64,4]{1,2,0:T(4,128)(2,1)}, u32[]{:S(2)}) copy-start(bf16[8,64,4]{1,2,0:T(4,128)(2,1)} %param.11) | copy-start | bytes 12292
  4.0 53.6 %copy-start.1 = (bf16[584,512]{1,0:T(8,128)(2,1)S(1)}, bf16[584,512]{1,0:T(8,128)(2,1)}, u32[]{:S(2)}) copy-start(bf16[584,512]{1,0:T(8,128)(2,1)} %pack_cache.1.refs_1_) | copy-start | bytes 1794052
  4.0 16.8 %collective-permute-start.4 = (bf16[584,512]{1,0:T(8,128)(2,1)}, bf16[584,512]{1,0:T(8,128)(2,1)S(1)}, u32[]{:S(2)}, u32[]{:S(2)}) collective-permute-start(bf16[584,512]{1,0:T(8,128)(2,1)} %pack_cache.1.refs_1_), channel_id=1, source_target_pairs={{0,2},{1,7},{2,4},{3,1},{4,6},{5,3},{6,0},{7,5},{8,10},{9,15},{10,... | collective-permute-start | bytes 1794056 | tf_op jit(solution)/shard_map/ppermute | solution.py:286
  5.6 29.1 %collective-permute-start.5 = (bf16[584,512]{1,0:T(8,128)(2,1)}, bf16[584,512]{1,0:T(8,128)(2,1)S(1)}, u32[]{:S(2)}, u32[]{:S(2)}) collective-permute-start(bf16[584,512]{1,0:T(8,128)(2,1)} %pack_cache.1.refs_1_), channel_id=1, source_target_pairs={{0,6},{1,3},{2,0},{3,5},{4,2},{5,7},{6,4},{7,1},{8,14},{9,11},{10,... | collective-permute-start | bytes 1794056 | tf_op jit(solution)/shard_map/ppermute | solution.py:286
  20.9 14.3 %collective-permute-start.6 = (bf16[584,512]{1,0:T(8,128)(2,1)S(1)}, bf16[584,512]{1,0:T(8,128)(2,1)S(1)}, u32[]{:S(2)}, u32[]{:S(2)}) collective-permute-start(bf16[584,512]{1,0:T(8,128)(2,1)S(1)} %collective-permute-done.4.refs_2_), channel_id=1, source_target_pairs={{0,2},{1,7},{2,4},{3,1},{4,6},{5,3},{6,0},{7,5},{8,10},{9,15},{10,... | collective-permute-start | bytes 1794056 | tf_op jit(solution)/shard_map/ppermute | solution.py:286
  21.3 32.2 %collective-permute-start.7 = (bf16[584,512]{1,0:T(8,128)(2,1)}, bf16[584,512]{1,0:T(8,128)(2,1)S(1)}, u32[]{:S(2)}, u32[]{:S(2)}) collective-permute-start(bf16[584,512]{1,0:T(8,128)(2,1)} %pack_cache.1.refs_1_), channel_id=1, source_target_pairs={{0,1},{1,0},{2,3},{3,2},{4,5},{5,4},{6,7},{7,6},{8,9},{9,8},{10,11... | collective-permute-start | bytes 1794056 | tf_op jit(solution)/shard_map/ppermute | solution.py:304
  21.4 4.1 %collective-permute-start = (bf16[1,144,128]{2,1,0:T(8,128)(2,1)S(1)}, bf16[1,144,128]{2,1,0:T(8,128)(2,1)S(1)}, u32[]{:S(2)}, u32[]{:S(2)}) collective-permute-start(bf16[1,144,128]{2,1,0:T(8,128)(2,1)S(1)} %pack_query.1.q_ref), channel_id=1, source_target_pairs={{0,32},{32,0},{64,96},{96,64},{128,160},{160,128},{192,224},{224,1... | collective-permute-start | bytes 110600 | tf_op jit(solution)/shard_map/ppermute | solution.py:295
  25.5 9.2 %collective-permute-start.1 = (bf16[2,144,128]{2,1,0:T(8,128)(2,1)S(1)}, bf16[2,144,128]{2,1,0:T(8,128)(2,1)S(1)}, u32[]{:S(2)}, u32[]{:S(2)}) collective-permute-start(bf16[2,144,128]{2,1,0:T(8,128)(2,1)S(1)} %pad_maximum_fusion), channel_id=1, source_target_pairs={{0,64},{32,96},{64,128},{96,160},{128,192},{160,224},{192,0},{224,... | collective-permute-start | bytes 221192 | tf_op jit(solution)/shard_map/ppermute | solution.py:300
  28.9 10.2 %collective-permute-start.2 = (bf16[2,144,128]{2,1,0:T(8,128)(2,1)S(1)}, bf16[2,144,128]{2,1,0:T(8,128)(2,1)S(1)}, u32[]{:S(2)}, u32[]{:S(2)}) collective-permute-start(bf16[2,144,128]{2,1,0:T(8,128)(2,1)S(1)} %pad_maximum_fusion), channel_id=1, source_target_pairs={{0,128},{32,160},{64,192},{96,224},{128,0},{160,32},{192,64},{224,... | collective-permute-start | bytes 221192 | tf_op jit(solution)/shard_map/ppermute | solution.py:300
  34.7 22.9 %collective-permute-start.8 = (bf16[584,512]{1,0:T(8,128)(2,1)S(1)}, bf16[584,512]{1,0:T(8,128)(2,1)S(1)}, u32[]{:S(2)}, u32[]{:S(2)}) collective-permute-start(bf16[584,512]{1,0:T(8,128)(2,1)S(1)} %collective-permute-done.4.refs_2_), channel_id=1, source_target_pairs={{0,1},{1,0},{2,3},{3,2},{4,5},{5,4},{6,7},{7,6},{8,9},{9,8},{10,11... | collective-permute-start | bytes 1794056 | tf_op jit(solution)/shard_map/ppermute | solution.py:304
  34.7 22.9 %collective-permute-start.9 = (bf16[584,512]{1,0:T(8,128)(2,1)S(1)}, bf16[584,512]{1,0:T(8,128)(2,1)S(1)}, u32[]{:S(2)}, u32[]{:S(2)}) collective-permute-start(bf16[584,512]{1,0:T(8,128)(2,1)S(1)} %collective-permute-done.5.refs_3_), channel_id=1, source_target_pairs={{0,1},{1,0},{2,3},{3,2},{4,5},{5,4},{6,7},{7,6},{8,9},{9,8},{10,11... | collective-permute-start | bytes 1794056 | tf_op jit(solution)/shard_map/ppermute | solution.py:304
  35.2 22.4 %collective-permute-start.10 = (bf16[584,512]{1,0:T(8,128)(2,1)S(1)}, bf16[584,512]{1,0:T(8,128)(2,1)S(1)}, u32[]{:S(2)}, u32[]{:S(2)}) collective-permute-start(bf16[584,512]{1,0:T(8,128)(2,1)S(1)} %collective-permute-done.6.refs_4_), channel_id=1, source_target_pairs={{0,1},{1,0},{2,3},{3,2},{4,5},{5,4},{6,7},{7,6},{8,9},{9,8},{10,11... | collective-permute-start | bytes 1794056 | tf_op jit(solution)/shard_map/ppermute | solution.py:304
  39.1 6.0 %collective-permute-start.3 = (bf16[2,144,128]{2,1,0:T(8,128)(2,1)S(1)}, bf16[2,144,128]{2,1,0:T(8,128)(2,1)S(1)}, u32[]{:S(2)}, u32[]{:S(2)}) collective-permute-start(bf16[2,144,128]{2,1,0:T(8,128)(2,1)S(1)} %pad_maximum_fusion), channel_id=1, source_target_pairs={{0,192},{32,224},{64,0},{96,32},{128,64},{160,96},{192,128},{224,1... | collective-permute-start | bytes 221192 | tf_op jit(solution)/shard_map/ppermute | solution.py:300
  45.1 7.3 %collective-permute-start.15 = (bf16[8,144,128]{2,1,0:T(8,128)(2,1)S(1)}, bf16[8,144,128]{2,1,0:T(8,128)(2,1)S(1)}, u32[]{:S(2)}, u32[]{:S(2)}) collective-permute-start(bf16[8,144,128]{2,1,0:T(8,128)(2,1)S(1)} %constant_dynamic-update-slice_fusion.refs_0_), channel_id=1, source_target_pairs={{0,24},{1,9},{8,0},{9,17},{16,8},{17,25},{24,16},{25,1},{2,26},{3,... | collective-permute-start | bytes 884744 | tf_op jit(solution)/shard_map/ppermute | solution.py:286
  52.4 10.5 %collective-permute-start.13 = (bf16[8,144,128]{2,1,0:T(8,128)(2,1)S(1)}, bf16[8,144,128]{2,1,0:T(8,128)(2,1)S(1)}, u32[]{:S(2)}, u32[]{:S(2)}) collective-permute-start(bf16[8,144,128]{2,1,0:T(8,128)(2,1)S(1)} %constant_dynamic-update-slice_fusion.refs_0_), channel_id=1, source_target_pairs={{0,8},{1,25},{8,16},{9,1},{16,24},{17,9},{24,0},{25,17},{2,10},{3,... | collective-permute-start | bytes 884744 | tf_op jit(solution)/shard_map/ppermute | solution.py:286
  53.5 14.8 %collective-permute-start.11 = (bf16[8,144,128]{2,1,0:T(8,128)(2,1)S(1)}, bf16[8,144,128]{2,1,0:T(8,128)(2,1)S(1)}, u32[]{:S(2)}, u32[]{:S(2)}) collective-permute-start(bf16[8,144,128]{2,1,0:T(8,128)(2,1)S(1)} %constant_dynamic-update-slice_fusion.refs_0_), channel_id=1, source_target_pairs={{0,16},{8,24},{16,0},{24,8},{1,17},{9,25},{17,1},{25,9},{2,18},{10... | collective-permute-start | bytes 884744 | tf_op jit(solution)/shard_map/ppermute | solution.py:291
  61.2 14.3 %collective-permute-start.16 = (bf16[8,136,128]{2,1,0:T(8,128)(2,1)S(1)}, bf16[8,136,128]{2,1,0:T(8,128)(2,1)S(1)}, u32[]{:S(2)}, u32[]{:S(2)}) collective-permute-start(bf16[8,136,128]{2,1,0:T(8,128)(2,1)S(1)} %attend.7), channel_id=1, source_target_pairs={{0,8},{1,25},{8,16},{9,1},{16,24},{17,9},{24,0},{25,17},{2,10},{3,... | collective-permute-start | bytes 835592 | tf_op jit(solution)/shard_map/ppermute | solution.py:286
  66.5 9.0 %collective-permute-start.14 = (bf16[8,136,128]{2,1,0:T(8,128)(2,1)S(1)}, bf16[8,136,128]{2,1,0:T(8,128)(2,1)S(1)}, u32[]{:S(2)}, u32[]{:S(2)}) collective-permute-start(bf16[8,136,128]{2,1,0:T(8,128)(2,1)S(1)} %attend.6), channel_id=1, source_target_pairs={{0,24},{1,9},{8,0},{9,17},{16,8},{17,25},{24,16},{25,1},{2,26},{3,... | collective-permute-start | bytes 835592 | tf_op jit(solution)/shard_map/ppermute | solution.py:286
  71.8 8.1 %collective-permute-start.12 = (bf16[8,136,128]{2,1,0:T(8,128)(2,1)S(1)}, bf16[8,136,128]{2,1,0:T(8,128)(2,1)S(1)}, u32[]{:S(2)}, u32[]{:S(2)}) collective-permute-start(bf16[8,136,128]{2,1,0:T(8,128)(2,1)S(1)} %get-tuple-element.4), channel_id=1, source_target_pairs={{0,16},{8,24},{16,0},{24,8},{1,17},{9,25},{17,1},{25,9},{2,18},{10... | collective-permute-start | bytes 835592 | tf_op jit(solution)/shard_map/ppermute | solution.py:291
  81.0 24.0 %copy-start.2 = (bf16[4,512,128]{2,1,0:T(8,128)(2,1)S(1)}, bf16[4,512,128]{2,1,0:T(8,128)(2,1)}, u32[]{:S(2)}) copy-start(bf16[4,512,128]{2,1,0:T(8,128)(2,1)} %w_ref.1) | copy-start | bytes 1572868
  81.0 24.0 %copy-start.3 = (bf16[64,512]{1,0:T(8,128)(2,1)S(1)}, bf16[64,512]{1,0:T(8,128)(2,1)}, u32[]{:S(2)}) copy-start(bf16[64,512]{1,0:T(8,128)(2,1)} %d_lat_ref.1) | copy-start | bytes 196612
  81.0 24.0 %all-to-all-start = ((bf16[8,136,128]{2,1,0:T(8,128)(2,1)}), bf16[8,136,128]{2,1,0:T(8,128)(2,1)S(1)}, u32[]{:S(2)}, u32[]{:S(2)}) async-start(bf16[8,136,128]{2,1,0:T(8,128)(2,1)} %merge.1), calls=%async_computation | async-start | bytes 557056 | tf_op jit(solution)/shard_map/all_to_all | solution.py:348
  94.4 10.7 %copy-start.5 = (bf16[64,64]{1,0:T(8,128)(2,1)S(1)}, bf16[64,64]{1,0:T(8,128)(2,1)}, u32[]{:S(2)}) copy-start(bf16[64,64]{1,0:T(8,128)(2,1)} %d_rope_ref.1) | copy-start | bytes 24580

commit v2 on v1

--- a/solution.py
+++ b/solution.py
@@ -41,7 +41,7 @@
 def attend_kernel(n_queries, n_chunks, counted, *refs):
     q_refs, chunks = refs[:n_queries], refs[n_queries : n_queries + n_chunks]
     out_ref = refs[n_queries + n_chunks]
-    query, query_rope, scores = refs[-3:]
+    query, query_rope, scores, weights = refs[-4:]
     rows = LATENT
     lane = lax.broadcasted_iota(jnp.int32, (BLOCK, LANES), 1)
     query_rope[...] = jnp.where(lane == ROPE, 1.0, 0.0).astype(jnp.bfloat16)
@@ -61,26 +61,48 @@
         both = owners[i][4 * ROWS :, :]
         query_rope[i * ROWS : i * ROWS + 16, :ROPE] = both[:, :ROPE]
         query_rope[i * ROWS + 16 : (i + 1) * ROWS, :ROPE] = both[:, ROPE:]
-    peak = None
-    for c in range(n_chunks):
-        here = slice(c * rows, (c + 1) * rows)
+    half = n_chunks // 2
+
+    def score(c):
         s = dot(query[...], chunks[c][:rows, :], ((1,), (1,)))
         s = s + dot(query_rope[:, : ROPE + EXTRA], chunks[c][rows:, :])
-        scores[:, here] = s
-        for j in range(rows // LANES):
-            part = s[:, j * LANES : (j + 1) * LANES]
-            peak = part if peak is None else jnp.maximum(peak, part)
-    peak = jnp.max(peak, axis=1, keepdims=True)
-    total = jnp.zeros((BLOCK, LANES), jnp.float32)
-    latent = jnp.zeros((BLOCK, LATENT), jnp.float32)
-    for c in range(n_chunks):
-        here = slice(c * rows, (c + 1) * rows)
-        p = jnp.exp2((scores[:, here] - peak) * SCALE2)
-        for j in range(rows // LANES):
-            total = total + p[:, j * LANES : (j + 1) * LANES]
-        latent = latent + dot(p.astype(jnp.bfloat16), chunks[c][:rows, :])
-    total = jnp.sum(total, axis=1, keepdims=True)
-    latent = (latent * (1.0 / total)).astype(jnp.bfloat16)
+        scores[:, c * rows : (c + 1) * rows] = s
+        tiles = [s[:, j * LANES : (j + 1) * LANES] for j in range(rows // LANES)]
+        return functools.reduce(jnp.maximum, tiles)
+
+    def weigh(c, peak):
+        p = jnp.exp2((scores[:, c * rows : (c + 1) * rows] - peak) * SCALE2)
+        weights[:, c * rows : (c + 1) * rows] = p.astype(jnp.bfloat16)
+        tiles = [p[:, j * LANES : (j + 1) * LANES] for j in range(rows // LANES)]
+        return sum(tiles[1:], tiles[0])
+
+    def value(c):
+        return dot(weights[:, c * rows : (c + 1) * rows], chunks[c][:rows, :])
+
+    peak_a = functools.reduce(jnp.maximum, [score(c) for c in range(half)])
+    peak_a = jnp.max(peak_a, axis=1, keepdims=True)
+    peak_b, total_a = None, None
+    for c in range(half):
+        part = score(half + c)
+        peak_b = part if peak_b is None else jnp.maximum(peak_b, part)
+        part = weigh(c, peak_a)
+        total_a = part if total_a is None else total_a + part
+    peak_b = jnp.max(peak_b, axis=1, keepdims=True)
+    latent_a, total_b = None, None
+    for c in range(half):
+        part = value(c)
+        latent_a = part if latent_a is None else latent_a + part
+        part = weigh(half + c, peak_b)
+        total_b = part if total_b is None else total_b + part
+    latent_b = sum((value(c) for c in range(half + 1, n_chunks)), value(half))
+    peak = jnp.maximum(peak_a, peak_b)
+    keep_a = jnp.exp2((peak_a - peak) * SCALE2)
+    keep_b = jnp.exp2((peak_b - peak) * SCALE2)
+    total_a = jnp.sum(total_a, axis=1, keepdims=True) * keep_a
+    total_b = jnp.sum(total_b, axis=1, keepdims=True) * keep_b
+    total = total_a + total_b
+    latent = latent_a * (keep_a / total) + latent_b * (keep_b / total)
+    latent = latent.astype(jnp.bfloat16)
     lse = peak * SCALE2 + jnp.log2(total)
     for i in range(OWNERS):
         mine = slice(i * ROWS, (i + 1) * ROWS)
@@ -111,8 +133,9 @@
             pltpu.VMEM((BLOCK, LATENT), jnp.bfloat16),
             pltpu.VMEM((BLOCK, LANES), jnp.bfloat16),
             pltpu.VMEM((BLOCK, n * LATENT), jnp.float32),
+            pltpu.VMEM((BLOCK, n * LATENT), jnp.bfloat16),
         ],
-        compiler_params=pltpu.CompilerParams(vmem_limit_bytes=12 * 2**20),
+        compiler_params=pltpu.CompilerParams(vmem_limit_bytes=14 * 2**20),
         cost_estimate=pl.CostEstimate(
             flops=BLOCK * n * LATENT * 2 * 1280, bytes_accessed=2**20, transcendentals=0
         ),
@@ -189,32 +212,57 @@
     )(q_latent, q_rope)
 
 
-def pack_cache_kernel(valid_ref, accepted_ref, lat, rope, out_ref, sems):
-    copies = [
-        pltpu.make_async_copy(lat, out_ref.at[:LATENT], sems.at[0]),
-        pltpu.make_async_copy(rope, out_ref.at[LATENT : LATENT + ROPE], sems.at[1]),
+def pack_cache_kernel(valid, accepted, lat, rope, out, packed, valid_ref, accepted_ref, sems):
+    parts = 4
+    step = LATENT // parts
+    spans = [slice(i * step, (i + 1) * step) for i in range(parts)]
+    loads = [
+        pltpu.make_async_copy(lat.at[span], packed.at[span], sems.at[i])
+        for i, span in enumerate(spans)
     ]
-    for copy in copies:
+    last = slice(LATENT, LATENT + ROPE + EXTRA)
+    rest = [
+        pltpu.make_async_copy(rope, packed.at[LATENT : LATENT + ROPE], sems.at[parts]),
+        pltpu.make_async_copy(valid, valid_ref, sems.at[parts + 1]),
+        pltpu.make_async_copy(accepted, accepted_ref, sems.at[parts + 2]),
+    ]
+    stores = [
+        pltpu.make_async_copy(packed.at[span], out.at[span], sems.at[parts + 3 + i])
+        for i, span in enumerate(spans + [last])
+    ]
+    for copy in rest + loads:
         copy.start()
+    for copy in rest:
+        copy.wait()
     limit = valid_ref[0] - lax.axis_index(SEQ + BLK) * LATENT
     count = sum(accepted_ref[i] for i in range(accepted_ref.shape[0]))
     lane = lax.broadcasted_iota(jnp.int32, (EXTRA, LATENT), 1)
     row = lax.broadcasted_iota(jnp.int32, (EXTRA, LATENT), 0)
     dead = jnp.where((row == 0) & (lane >= limit), NEG, 0.0)
     extra = jnp.where(row == 1, count.astype(jnp.float32), dead)
-    out_ref[LATENT + ROPE :, :] = extra.astype(jnp.bfloat16)
-    copies[0].wait()
-    copies[1].wait()
+    packed[LATENT + ROPE :, :] = extra.astype(jnp.bfloat16)
+    for load, store in zip(loads, stores):
+        load.wait()
+        store.start()
+    stores[-1].start()
+    for store in stores:
+        store.wait()
 
 
 def pack_cache(valid_length, accepted, cache_latent, cache_rope):
+    hbm = pl.BlockSpec(memory_space=pltpu.HBM)
+    rows = LATENT + ROPE + EXTRA
     return pl.pallas_call(
         pack_cache_kernel,
-        out_shape=jax.ShapeDtypeStruct((LATENT + ROPE + EXTRA, LATENT), jnp.bfloat16),
-        in_specs=[pl.BlockSpec(memory_space=pltpu.SMEM)] * 2
-        + [pl.BlockSpec(memory_space=pltpu.HBM)] * 2,
-        out_specs=pl.BlockSpec(memory_space=pltpu.VMEM),
-        scratch_shapes=[pltpu.SemaphoreType.DMA((2,))],
+        out_shape=jax.ShapeDtypeStruct((rows, LATENT), jnp.bfloat16),
+        in_specs=[hbm] * 4,
+        out_specs=hbm,
+        scratch_shapes=[
+            pltpu.VMEM((rows, LATENT), jnp.bfloat16),
+            pltpu.SMEM((1,), jnp.int32),
+            pltpu.SMEM(accepted.shape, jnp.int32),
+            pltpu.SemaphoreType.DMA((12,)),
+        ],
         compiler_params=pltpu.CompilerParams(vmem_limit_bytes=60 * 1024 * 2**10 - 660 * 2**10),
         name="pack_cache",
     )(valid_length.reshape(1), accepted, cache_latent, cache_rope)

time: 108 us -> 107 us (level)
  the two profiles are of different devices: /device:TPU:2 before, /device:TPU:4 now
where the time goes in v2:
time: 107 us
  starting transfers between devices  42.9 us (40%)
  waiting for transfers between devices  42.5 us (40%)
  Pallas kernels  17.5 us (16%)
  between operations  3.23 us (3%)
    ppermute x7, waiting for transfers between devices, shift(): lax.ppermute(value, (axis, 'core'), both_ways(lax.axis_size(axis), step))  19.7 us
    all_to_all x1, starting transfers between devices, shards(): pieces = lax.all_to_all(pieces, 'z', 0, 0, tiled=True)  13.9 us
    pallas_call x4, Pallas kernels, attend(): pl.pallas_call(functools.partial(attend_kernel, len(queries), n, counted)...  13.1 us
    ppermute x3, starting transfers between devices, rotate(): return lax.ppermute(value, axis, [(i, (i + step) % n) for i in range(n)])  12.6 us
    ppermute x7, starting transfers between devices, shift(): lax.ppermute(value, (axis, 'core'), both_ways(lax.axis_size(axis), step))  9.6 us
    all_to_all x1, waiting for transfers between devices, shards(): pieces = lax.all_to_all(pieces, 'z', 0, 0, tiled=True)  9.46 us
    ppermute x3, waiting for transfers between devices, rotate(): return lax.ppermute(value, axis, [(i, (i + step) % n) for i in range(n)])  6.27 us
    ppermute x2, waiting for transfers between devices, across(): return lax.ppermute(value, axis, [(i, (i + n // 2) % n) for i in range(n)])  4.92 us
  transfers between devices with their start and end apart: 18, of which 9 were waited for; matrix products, arithmetic and copies ran while one was open for 1% of the time, Pallas kernels for 12%

profile of v2, /device:TPU:4, one launch (start us, length us, event | category | flops | bytes accessed | tf_op | source)
XLA Modules:
  0.0 106.7 jit_solution(6831794429753385937)
XLA Ops:
  1.3 1.9 %pack_cache.1.refs_1_ = bf16[584,512]{1,0:T(8,128)(2,1)} custom-call(s32[1]{0:T(128)} %bitcast.4.valid, s32[8]{0:T(128)} %accepted.1, bf16[512,512]{1,0:T(8,128)(2,1)} %lat.1, bf16[64,512]{1,0:T(8,128)(2,1)} %rope.1), custom_call_target="tpu_custom_call" | custom-call | tf_op jit(solution)/shard_map/pack_cache/pallas_call | solution.py:255
  3.3 1.3 %collective-permute-start.4 = (bf16[584,512]{1,0:T(8,128)(2,1)}, bf16[584,512]{1,0:T(8,128)(2,1)S(1)}, u32[]{:S(2)}, u32[]{:S(2)}) collective-permute-start(bf16[584,512]{1,0:T(8,128)(2,1)} %pack_cache.1.refs_1_), channel_id=1, source_target_pairs={{0,2},{1,7},{2,4},{3,1},{4,6},{5,3},{6,0},{7,5},{8,10},{9,15},{10,... | collective-permute-start | bytes 1794056 | tf_op jit(solution)/shard_map/ppermute | solution.py:334
  4.6 0.8 collective-permute-start.5
  5.4 13.7 %collective-permute-done.4.refs_2_ = bf16[584,512]{1,0:T(8,128)(2,1)S(1)} collective-permute-done((bf16[584,512]{1,0:T(8,128)(2,1)}, bf16[584,512]{1,0:T(8,128)(2,1)S(1)}, u32[]{:S(2)}, u32[]{:S(2)}) %collective-permute-start.4) | collective-permute-done | bytes 598048 | tf_op jit(solution)/shard_map/ppermute | solution.py:334
  19.1 1.5 %collective-permute-start.6 = (bf16[584,512]{1,0:T(8,128)(2,1)S(1)}, bf16[584,512]{1,0:T(8,128)(2,1)S(1)}, u32[]{:S(2)}, u32[]{:S(2)}) collective-permute-start(bf16[584,512]{1,0:T(8,128)(2,1)S(1)} %collective-permute-done.4.refs_2_), channel_id=1, source_target_pairs={{0,2},{1,7},{2,4},{3,1},{4,6},{5,3},{6,0},{7,5},{8,10},{9,15},{10,... | collective-permute-start | bytes 1794056 | tf_op jit(solution)/shard_map/ppermute | solution.py:334
  20.7 1.9 %collective-permute-start = (bf16[1,144,128]{2,1,0:T(8,128)(2,1)S(1)}, bf16[1,144,128]{2,1,0:T(8,128)(2,1)S(1)}, u32[]{:S(2)}, u32[]{:S(2)}) collective-permute-start(bf16[1,144,128]{2,1,0:T(8,128)(2,1)S(1)} %pack_query.1.q_ref), channel_id=1, source_target_pairs={{0,32},{32,0},{64,96},{96,64},{128,160},{160,128},{192,224},{224,1... | collective-permute-start | bytes 110600 | tf_op jit(solution)/shard_map/ppermute | solution.py:343
  22.6 2.1 %collective-permute-done = bf16[1,144,128]{2,1,0:T(8,128)(2,1)S(1)} collective-permute-done((bf16[1,144,128]{2,1,0:T(8,128)(2,1)S(1)}, bf16[1,144,128]{2,1,0:T(8,128)(2,1)S(1)}, u32[]{:S(2)}, u32[]{:S(2)}) %collective-permute-start) | collective-permute-done | bytes 36896 | tf_op jit(solution)/shard_map/ppermute | solution.py:343
  24.8 3.3 %collective-permute-start.1 = (bf16[2,144,128]{2,1,0:T(8,128)(2,1)S(1)}, bf16[2,144,128]{2,1,0:T(8,128)(2,1)S(1)}, u32[]{:S(2)}, u32[]{:S(2)}) collective-permute-start(bf16[2,144,128]{2,1,0:T(8,128)(2,1)S(1)} %pad_maximum_fusion), channel_id=1, source_target_pairs={{0,64},{32,96},{64,128},{96,160},{128,192},{160,224},{192,0},{224,... | collective-permute-start | bytes 221192 | tf_op jit(solution)/shard_map/ppermute | solution.py:348
  28.1 5.3 %collective-permute-start.2 = (bf16[2,144,128]{2,1,0:T(8,128)(2,1)S(1)}, bf16[2,144,128]{2,1,0:T(8,128)(2,1)S(1)}, u32[]{:S(2)}, u32[]{:S(2)}) collective-permute-start(bf16[2,144,128]{2,1,0:T(8,128)(2,1)S(1)} %pad_maximum_fusion), channel_id=1, source_target_pairs={{0,128},{32,160},{64,192},{96,224},{128,0},{160,32},{192,64},{224,... | collective-permute-start | bytes 221192 | tf_op jit(solution)/shard_map/ppermute | solution.py:348
  33.4 0.5 collective-permute-done.1
  33.9 0.5 collective-permute-start.9
  34.5 3.8 %collective-permute-done.2 = bf16[2,144,128]{2,1,0:T(8,128)(2,1)S(1)} collective-permute-done((bf16[2,144,128]{2,1,0:T(8,128)(2,1)S(1)}, bf16[2,144,128]{2,1,0:T(8,128)(2,1)S(1)}, u32[]{:S(2)}, u32[]{:S(2)}) %collective-permute-start.2) | collective-permute-done | bytes 73760 | tf_op jit(solution)/shard_map/ppermute | solution.py:348
  38.3 4.0 %collective-permute-start.3 = (bf16[2,144,128]{2,1,0:T(8,128)(2,1)S(1)}, bf16[2,144,128]{2,1,0:T(8,128)(2,1)S(1)}, u32[]{:S(2)}, u32[]{:S(2)}) collective-permute-start(bf16[2,144,128]{2,1,0:T(8,128)(2,1)S(1)} %pad_maximum_fusion), channel_id=1, source_target_pairs={{0,192},{32,224},{64,0},{96,32},{128,64},{160,96},{192,128},{224,1... | collective-permute-start | bytes 221192 | tf_op jit(solution)/shard_map/ppermute | solution.py:348
  42.4 2.0 %collective-permute-done.3 = bf16[2,144,128]{2,1,0:T(8,128)(2,1)S(1)} collective-permute-done((bf16[2,144,128]{2,1,0:T(8,128)(2,1)S(1)}, bf16[2,144,128]{2,1,0:T(8,128)(2,1)S(1)}, u32[]{:S(2)}, u32[]{:S(2)}) %collective-permute-start.3) | collective-permute-done | bytes 73760 | tf_op jit(solution)/shard_map/ppermute | solution.py:348
  44.3 3.1 %collective-permute-start.15 = (bf16[8,144,128]{2,1,0:T(8,128)(2,1)S(1)}, bf16[8,144,128]{2,1,0:T(8,128)(2,1)S(1)}, u32[]{:S(2)}, u32[]{:S(2)}) collective-permute-start(bf16[8,144,128]{2,1,0:T(8,128)(2,1)S(1)} %constant_dynamic-update-slice_fusion.refs_0_), channel_id=1, source_target_pairs={{0,24},{1,9},{8,0},{9,17},{16,8},{17,25},{24,16},{25,1},{2,26},{3,... | collective-permute-start | bytes 884744 | tf_op jit(solution)/shard_map/ppermute | solution.py:334
  47.4 4.2 %collective-permute-done.15.refs_0_ = bf16[8,144,128]{2,1,0:T(8,128)(2,1)S(1)} collective-permute-done((bf16[8,144,128]{2,1,0:T(8,128)(2,1)S(1)}, bf16[8,144,128]{2,1,0:T(8,128)(2,1)S(1)}, u32[]{:S(2)}, u32[]{:S(2)}) %collective-permute-start.15) | collective-permute-done | bytes 294944 | tf_op jit(solution)/shard_map/ppermute | solution.py:334
  51.7 1.0 collective-permute-start.13
  52.7 4.1 %collective-permute-start.11 = (bf16[8,144,128]{2,1,0:T(8,128)(2,1)S(1)}, bf16[8,144,128]{2,1,0:T(8,128)(2,1)S(1)}, u32[]{:S(2)}, u32[]{:S(2)}) collective-permute-start(bf16[8,144,128]{2,1,0:T(8,128)(2,1)S(1)} %constant_dynamic-update-slice_fusion.refs_0_), channel_id=1, source_target_pairs={{0,16},{8,24},{16,0},{24,8},{1,17},{9,25},{17,1},{25,9},{2,18},{10... | collective-permute-start | bytes 884744 | tf_op jit(solution)/shard_map/ppermute | solution.py:339
  56.9 3.3 %attend.7 = bf16[8,136,128]{2,1,0:T(8,128)(2,1)S(1)} custom-call(bf16[8,144,128]{2,1,0:T(8,128)(2,1)S(1)} %collective-permute-done.15.refs_0_, bf16[584,512]{1,0:T(8,128)(2,1)S(1)} %copy-done.1, bf16[584,512]{1,0:T(8,128)(2,1)S(1)} %collective-permute-done.4.refs_2_, bf16[584,512]{1,0:T(8,128)(2,1)S(1)} %collective-permute-done.5.refs_3_, ...), custom_call_target="tpu_custom_call" | custom-call | flops 2684354560 | bytes 1048576 | tf_op jit(solution)/shard_map/attend/pallas_call | solution.py:124
  60.2 0.3 collective-permute-start.16
  60.4 1.7 %collective-permute-done.13.refs_0_ = bf16[8,144,128]{2,1,0:T(8,128)(2,1)S(1)} collective-permute-done((bf16[8,144,128]{2,1,0:T(8,128)(2,1)S(1)}, bf16[8,144,128]{2,1,0:T(8,128)(2,1)S(1)}, u32[]{:S(2)}, u32[]{:S(2)}) %collective-permute-start.13) | collective-permute-done | bytes 294944 | tf_op jit(solution)/shard_map/ppermute | solution.py:334
  62.2 3.3 %attend.6 = bf16[8,136,128]{2,1,0:T(8,128)(2,1)S(1)} custom-call(bf16[8,144,128]{2,1,0:T(8,128)(2,1)S(1)} %collective-permute-done.13.refs_0_, bf16[584,512]{1,0:T(8,128)(2,1)S(1)} %copy-done.1, bf16[584,512]{1,0:T(8,128)(2,1)S(1)} %collective-permute-done.4.refs_2_, bf16[584,512]{1,0:T(8,128)(2,1)S(1)} %collective-permute-done.5.refs_3_, ...), custom_call_target="tpu_custom_call" | custom-call | flops 2684354560 | bytes 1048576 | tf_op jit(solution)/shard_map/attend/pallas_call | solution.py:124
  65.5 1.6 %collective-permute-start.14 = (bf16[8,136,128]{2,1,0:T(8,128)(2,1)S(1)}, bf16[8,136,128]{2,1,0:T(8,128)(2,1)S(1)}, u32[]{:S(2)}, u32[]{:S(2)}) collective-permute-start(bf16[8,136,128]{2,1,0:T(8,128)(2,1)S(1)} %attend.6), channel_id=1, source_target_pairs={{0,24},{1,9},{8,0},{9,17},{16,8},{17,25},{24,16},{25,1},{2,26},{3,... | collective-permute-start | bytes 835592 | tf_op jit(solution)/shard_map/ppermute | solution.py:334
  67.0 3.3 %attend.5 = (bf16[8,136,128]{2,1,0:T(8,128)(2,1)S(1)}, f32[8,128]{1,0:T(8,128)S(1)}) custom-call(bf16[8,144,128]{2,1,0:T(8,128)(2,1)S(1)} %collective-permute-done.11.refs_0_, bf16[584,512]{1,0:T(8,128)(2,1)S(1)} %copy-done.1, bf16[584,512]{1,0:T(8,128)(2,1)S(1)} %collective-permute-done.4.refs_2_, bf16[584,512]{1,0:T(8,128)(2,1)S(1)} %collective-permute-done.5.refs_3_, ...), custom_call_target="tpu_custom_call" | custom-call | flops 2684354560 | bytes 1048576 | tf_op jit(solution)/shard_map/attend/pallas_call | solution.py:124
  70.3 0.2 collective-permute-start.12
  70.5 3.3 %attend.4.refs_0_ = bf16[8,136,128]{2,1,0:T(8,128)(2,1)S(1)} custom-call(bf16[8,144,128]{2,1,0:T(8,128)(2,1)S(1)} %constant_dynamic-update-slice_fusion.refs_0_, bf16[584,512]{1,0:T(8,128)(2,1)S(1)} %copy-done.1, bf16[584,512]{1,0:T(8,128)(2,1)S(1)} %collective-permute-done.4.refs_2_, bf16[584,512]{1,0:T(8,128)(2,1)S(1)} %collective-permute-done.5.refs_3_, ...), custom_call_target="tpu_custom_call" | custom-call | flops 2684354560 | bytes 1048576 | tf_op jit(solution)/shard_map/attend/pallas_call | solution.py:124
  73.8 4.9 %collective-permute-done.12.refs_1_ = bf16[8,136,128]{2,1,0:T(8,128)(2,1)S(1)} collective-permute-done((bf16[8,136,128]{2,1,0:T(8,128)(2,1)S(1)}, bf16[8,136,128]{2,1,0:T(8,128)(2,1)S(1)}, u32[]{:S(2)}, u32[]{:S(2)}) %collective-permute-start.12) | collective-permute-done | bytes 278560 | tf_op jit(solution)/shard_map/ppermute | solution.py:339
  78.7 1.0 merge.1
  79.7 13.9 %all-to-all-start = ((bf16[8,136,128]{2,1,0:T(8,128)(2,1)}), bf16[8,136,128]{2,1,0:T(8,128)(2,1)S(1)}, u32[]{:S(2)}, u32[]{:S(2)}) async-start(bf16[8,136,128]{2,1,0:T(8,128)(2,1)} %merge.1), calls=%async_computation | async-start | bytes 557056 | tf_op jit(solution)/shard_map/all_to_all | solution.py:396
  93.6 0.5 slice.3
  94.8 9.5 %all-to-all-done.pieces_ref = bf16[8,136,128]{2,1,0:T(8,128)(2,1)S(1)} async-done(((bf16[8,136,128]{2,1,0:T(8,128)(2,1)}), bf16[8,136,128]{2,1,0:T(8,128)(2,1)S(1)}, u32[]{:S(2)}, u32[]{:S(2)}) %all-to-all-start) | async-done | bytes 278560 | tf_op jit(solution)/shard_map/all_to_all | solution.py:396
  104.3 1.3 %finish.1 = bf16[8,4,128]{2,1,0:T(4,128)(2,1)} custom-call(bf16[8,136,128]{2,1,0:T(8,128)(2,1)S(1)} %all-to-all-done.pieces_ref, bf16[1,144,128]{2,1,0:T(8,128)(2,1)S(1)} %pack_query.1.q_ref, bf16[64,512]{1,0:T(8,128)(2,1)S(1)} %copy-done.3, bf16[64,64]{1,0:T(8,128)(2,1)S(1)} %copy-done.5, s32[32,64]{1,0:T(8,128)S(1)} %bitcast.5, ...), custom_call_target="tpu_custom_call" | custom-call | tf_op jit(solution)/shard_map/finish/pallas_call | solution.py:315
  (35 shorter events, 0.3 us)
Async XLA Ops:
  0.6 93.0 %copy-start = (s32[64,64]{1,0:T(8,128)S(1)}, s32[64,64]{1,0:T(8,128)}, u32[]{:S(2)}) copy-start(s32[64,64]{1,0:T(8,128)} %param.16) | copy-start | bytes 49156
  1.3 19.3 %copy-start.4 = (bf16[8,4,512]{2,1,0:T(4,128)(2,1)S(1)}, bf16[8,4,512]{2,1,0:T(4,128)(2,1)}, u32[]{:S(2)}) copy-start(bf16[8,4,512]{2,1,0:T(4,128)(2,1)} %lat_ref.1) | copy-start | bytes 98308
  1.3 19.3 %copy-start.6 = (bf16[8,64,4]{1,2,0:T(4,128)(2,1)S(1)}, bf16[8,64,4]{1,2,0:T(4,128)(2,1)}, u32[]{:S(2)}) copy-start(bf16[8,64,4]{1,2,0:T(4,128)(2,1)} %param.11) | copy-start | bytes 12292
  3.3 53.6 %copy-start.1 = (bf16[584,512]{1,0:T(8,128)(2,1)S(1)}, bf16[584,512]{1,0:T(8,128)(2,1)}, u32[]{:S(2)}) copy-start(bf16[584,512]{1,0:T(8,128)(2,1)} %pack_cache.1.refs_1_) | copy-start | bytes 1794052
  3.3 15.8 %collective-permute-start.4 = (bf16[584,512]{1,0:T(8,128)(2,1)}, bf16[584,512]{1,0:T(8,128)(2,1)S(1)}, u32[]{:S(2)}, u32[]{:S(2)}) collective-permute-start(bf16[584,512]{1,0:T(8,128)(2,1)} %pack_cache.1.refs_1_), channel_id=1, source_target_pairs={{0,2},{1,7},{2,4},{3,1},{4,6},{5,3},{6,0},{7,5},{8,10},{9,15},{10,... | collective-permute-start | bytes 1794056 | tf_op jit(solution)/shard_map/ppermute | solution.py:334
  4.6 29.4 %collective-permute-start.5 = (bf16[584,512]{1,0:T(8,128)(2,1)}, bf16[584,512]{1,0:T(8,128)(2,1)S(1)}, u32[]{:S(2)}, u32[]{:S(2)}) collective-permute-start(bf16[584,512]{1,0:T(8,128)(2,1)} %pack_cache.1.refs_1_), channel_id=1, source_target_pairs={{0,6},{1,3},{2,0},{3,5},{4,2},{5,7},{6,4},{7,1},{8,14},{9,11},{10,... | collective-permute-start | bytes 1794056 | tf_op jit(solution)/shard_map/ppermute | solution.py:334
  19.1 15.4 %collective-permute-start.6 = (bf16[584,512]{1,0:T(8,128)(2,1)S(1)}, bf16[584,512]{1,0:T(8,128)(2,1)S(1)}, u32[]{:S(2)}, u32[]{:S(2)}) collective-permute-start(bf16[584,512]{1,0:T(8,128)(2,1)S(1)} %collective-permute-done.4.refs_2_), channel_id=1, source_target_pairs={{0,2},{1,7},{2,4},{3,1},{4,6},{5,3},{6,0},{7,5},{8,10},{9,15},{10,... | collective-permute-start | bytes 1794056 | tf_op jit(solution)/shard_map/ppermute | solution.py:334
  20.6 32.1 %collective-permute-start.7 = (bf16[584,512]{1,0:T(8,128)(2,1)}, bf16[584,512]{1,0:T(8,128)(2,1)S(1)}, u32[]{:S(2)}, u32[]{:S(2)}) collective-permute-start(bf16[584,512]{1,0:T(8,128)(2,1)} %pack_cache.1.refs_1_), channel_id=1, source_target_pairs={{0,1},{1,0},{2,3},{3,2},{4,5},{5,4},{6,7},{7,6},{8,9},{9,8},{10,11... | collective-permute-start | bytes 1794056 | tf_op jit(solution)/shard_map/ppermute | solution.py:352
  20.7 4.1 %collective-permute-start = (bf16[1,144,128]{2,1,0:T(8,128)(2,1)S(1)}, bf16[1,144,128]{2,1,0:T(8,128)(2,1)S(1)}, u32[]{:S(2)}, u32[]{:S(2)}) collective-permute-start(bf16[1,144,128]{2,1,0:T(8,128)(2,1)S(1)} %pack_query.1.q_ref), channel_id=1, source_target_pairs={{0,32},{32,0},{64,96},{96,64},{128,160},{160,128},{192,224},{224,1... | collective-permute-start | bytes 110600 | tf_op jit(solution)/shard_map/ppermute | solution.py:343
  24.8 9.2 %collective-permute-start.1 = (bf16[2,144,128]{2,1,0:T(8,128)(2,1)S(1)}, bf16[2,144,128]{2,1,0:T(8,128)(2,1)S(1)}, u32[]{:S(2)}, u32[]{:S(2)}) collective-permute-start(bf16[2,144,128]{2,1,0:T(8,128)(2,1)S(1)} %pad_maximum_fusion), channel_id=1, source_target_pairs={{0,64},{32,96},{64,128},{96,160},{128,192},{160,224},{192,0},{224,... | collective-permute-start | bytes 221192 | tf_op jit(solution)/shard_map/ppermute | solution.py:348
  28.1 10.2 %collective-permute-start.2 = (bf16[2,144,128]{2,1,0:T(8,128)(2,1)S(1)}, bf16[2,144,128]{2,1,0:T(8,128)(2,1)S(1)}, u32[]{:S(2)}, u32[]{:S(2)}) collective-permute-start(bf16[2,144,128]{2,1,0:T(8,128)(2,1)S(1)} %pad_maximum_fusion), channel_id=1, source_target_pairs={{0,128},{32,160},{64,192},{96,224},{128,0},{160,32},{192,64},{224,... | collective-permute-start | bytes 221192 | tf_op jit(solution)/shard_map/ppermute | solution.py:348
  33.9 22.9 %collective-permute-start.8 = (bf16[584,512]{1,0:T(8,128)(2,1)S(1)}, bf16[584,512]{1,0:T(8,128)(2,1)S(1)}, u32[]{:S(2)}, u32[]{:S(2)}) collective-permute-start(bf16[584,512]{1,0:T(8,128)(2,1)S(1)} %collective-permute-done.4.refs_2_), channel_id=1, source_target_pairs={{0,1},{1,0},{2,3},{3,2},{4,5},{5,4},{6,7},{7,6},{8,9},{9,8},{10,11... | collective-permute-start | bytes 1794056 | tf_op jit(solution)/shard_map/ppermute | solution.py:352
  33.9 22.9 %collective-permute-start.9 = (bf16[584,512]{1,0:T(8,128)(2,1)S(1)}, bf16[584,512]{1,0:T(8,128)(2,1)S(1)}, u32[]{:S(2)}, u32[]{:S(2)}) collective-permute-start(bf16[584,512]{1,0:T(8,128)(2,1)S(1)} %collective-permute-done.5.refs_3_), channel_id=1, source_target_pairs={{0,1},{1,0},{2,3},{3,2},{4,5},{5,4},{6,7},{7,6},{8,9},{9,8},{10,11... | collective-permute-start | bytes 1794056 | tf_op jit(solution)/shard_map/ppermute | solution.py:352
  34.4 22.4 %collective-permute-start.10 = (bf16[584,512]{1,0:T(8,128)(2,1)S(1)}, bf16[584,512]{1,0:T(8,128)(2,1)S(1)}, u32[]{:S(2)}, u32[]{:S(2)}) collective-permute-start(bf16[584,512]{1,0:T(8,128)(2,1)S(1)} %collective-permute-done.6.refs_4_), channel_id=1, source_target_pairs={{0,1},{1,0},{2,3},{3,2},{4,5},{5,4},{6,7},{7,6},{8,9},{9,8},{10,11... | collective-permute-start | bytes 1794056 | tf_op jit(solution)/shard_map/ppermute | solution.py:352
  38.3 6.0 %collective-permute-start.3 = (bf16[2,144,128]{2,1,0:T(8,128)(2,1)S(1)}, bf16[2,144,128]{2,1,0:T(8,128)(2,1)S(1)}, u32[]{:S(2)}, u32[]{:S(2)}) collective-permute-start(bf16[2,144,128]{2,1,0:T(8,128)(2,1)S(1)} %pad_maximum_fusion), channel_id=1, source_target_pairs={{0,192},{32,224},{64,0},{96,32},{128,64},{160,96},{192,128},{224,1... | collective-permute-start | bytes 221192 | tf_op jit(solution)/shard_map/ppermute | solution.py:348
  44.3 7.3 %collective-permute-start.15 = (bf16[8,144,128]{2,1,0:T(8,128)(2,1)S(1)}, bf16[8,144,128]{2,1,0:T(8,128)(2,1)S(1)}, u32[]{:S(2)}, u32[]{:S(2)}) collective-permute-start(bf16[8,144,128]{2,1,0:T(8,128)(2,1)S(1)} %constant_dynamic-update-slice_fusion.refs_0_), channel_id=1, source_target_pairs={{0,24},{1,9},{8,0},{9,17},{16,8},{17,25},{24,16},{25,1},{2,26},{3,... | collective-permute-start | bytes 884744 | tf_op jit(solution)/shard_map/ppermute | solution.py:334
  51.7 10.5 %collective-permute-start.13 = (bf16[8,144,128]{2,1,0:T(8,128)(2,1)S(1)}, bf16[8,144,128]{2,1,0:T(8,128)(2,1)S(1)}, u32[]{:S(2)}, u32[]{:S(2)}) collective-permute-start(bf16[8,144,128]{2,1,0:T(8,128)(2,1)S(1)} %constant_dynamic-update-slice_fusion.refs_0_), channel_id=1, source_target_pairs={{0,8},{1,25},{8,16},{9,1},{16,24},{17,9},{24,0},{25,17},{2,10},{3,... | collective-permute-start | bytes 884744 | tf_op jit(solution)/shard_map/ppermute | solution.py:334
  52.7 14.3 %collective-permute-start.11 = (bf16[8,144,128]{2,1,0:T(8,128)(2,1)S(1)}, bf16[8,144,128]{2,1,0:T(8,128)(2,1)S(1)}, u32[]{:S(2)}, u32[]{:S(2)}) collective-permute-start(bf16[8,144,128]{2,1,0:T(8,128)(2,1)S(1)} %constant_dynamic-update-slice_fusion.refs_0_), channel_id=1, source_target_pairs={{0,16},{8,24},{16,0},{24,8},{1,17},{9,25},{17,1},{25,9},{2,18},{10... | collective-permute-start | bytes 884744 | tf_op jit(solution)/shard_map/ppermute | solution.py:339
  60.2 13.6 %collective-permute-start.16 = (bf16[8,136,128]{2,1,0:T(8,128)(2,1)S(1)}, bf16[8,136,128]{2,1,0:T(8,128)(2,1)S(1)}, u32[]{:S(2)}, u32[]{:S(2)}) collective-permute-start(bf16[8,136,128]{2,1,0:T(8,128)(2,1)S(1)} %attend.7), channel_id=1, source_target_pairs={{0,8},{1,25},{8,16},{9,1},{16,24},{17,9},{24,0},{25,17},{2,10},{3,... | collective-permute-start | bytes 835592 | tf_op jit(solution)/shard_map/ppermute | solution.py:334
  65.5 8.3 %collective-permute-start.14 = (bf16[8,136,128]{2,1,0:T(8,128)(2,1)S(1)}, bf16[8,136,128]{2,1,0:T(8,128)(2,1)S(1)}, u32[]{:S(2)}, u32[]{:S(2)}) collective-permute-start(bf16[8,136,128]{2,1,0:T(8,128)(2,1)S(1)} %attend.6), channel_id=1, source_target_pairs={{0,24},{1,9},{8,0},{9,17},{16,8},{17,25},{24,16},{25,1},{2,26},{3,... | collective-permute-start | bytes 835592 | tf_op jit(solution)/shard_map/ppermute | solution.py:334
  70.3 8.4 %collective-permute-start.12 = (bf16[8,136,128]{2,1,0:T(8,128)(2,1)S(1)}, bf16[8,136,128]{2,1,0:T(8,128)(2,1)S(1)}, u32[]{:S(2)}, u32[]{:S(2)}) collective-permute-start(bf16[8,136,128]{2,1,0:T(8,128)(2,1)S(1)} %get-tuple-element.4), channel_id=1, source_target_pairs={{0,16},{8,24},{16,0},{24,8},{1,17},{9,25},{17,1},{25,9},{2,18},{10... | collective-permute-start | bytes 835592 | tf_op jit(solution)/shard_map/ppermute | solution.py:339
  79.7 24.5 %copy-start.2 = (bf16[4,512,128]{2,1,0:T(8,128)(2,1)S(1)}, bf16[4,512,128]{2,1,0:T(8,128)(2,1)}, u32[]{:S(2)}) copy-start(bf16[4,512,128]{2,1,0:T(8,128)(2,1)} %w_ref.1) | copy-start | bytes 1572868
  79.7 24.5 %copy-start.3 = (bf16[64,512]{1,0:T(8,128)(2,1)S(1)}, bf16[64,512]{1,0:T(8,128)(2,1)}, u32[]{:S(2)}) copy-start(bf16[64,512]{1,0:T(8,128)(2,1)} %d_lat_ref.1) | copy-start | bytes 196612
  79.7 24.5 %all-to-all-start = ((bf16[8,136,128]{2,1,0:T(8,128)(2,1)}), bf16[8,136,128]{2,1,0:T(8,128)(2,1)S(1)}, u32[]{:S(2)}, u32[]{:S(2)}) async-start(bf16[8,136,128]{2,1,0:T(8,128)(2,1)} %merge.1), calls=%async_computation | async-start | bytes 557056 | tf_op jit(solution)/shard_map/all_to_all | solution.py:396
  93.6 10.7 %copy-start.5 = (bf16[64,64]{1,0:T(8,128)(2,1)S(1)}, bf16[64,64]{1,0:T(8,128)(2,1)}, u32[]{:S(2)}) copy-start(bf16[64,64]{1,0:T(8,128)(2,1)} %d_rope_ref.1) | copy-start | bytes 24580

commit v3 on v2

--- a/solution.py
+++ b/solution.py
@@ -268,12 +268,7 @@
     )(valid_length.reshape(1), accepted, cache_latent, cache_rope)
 
 
-def finish_kernel(tokens, heads, pieces_ref, q_ref, d_lat_ref, d_rope_ref, tree_ref, w_ref, out_ref):
-    pieces = [pieces_ref.at[i] for i in range(pieces_ref.shape[0])]
-    lses = []
-    for piece in pieces:
-        parts = piece[4 * ROWS :, :].astype(jnp.float32)
-        lses.append(parts[0:1, :] + parts[1:2, :] + parts[2:3, :])
+def draft_kernel(q_ref, d_lat_ref, d_rope_ref, tree_ref, latent_ref, peak_ref, total_ref):
     q_ref = q_ref.at[0]
     query = jnp.concatenate([q_ref[j * ROWS : (j + 1) * ROWS, :] for j in range(4)], axis=1)
     both = q_ref[4 * ROWS :, :]
@@ -281,24 +276,48 @@
     draft = d_lat_ref[...]
     score = dot(query, draft, ((1,), (1,))) + dot(query_rope, d_rope_ref[...])
     score = jnp.where(tree_ref[...] == 1, score * SCALE2, NEG)
-    draft_peak = jnp.max(score, axis=1, keepdims=True)
+    peak = jnp.max(score, axis=1, keepdims=True)
+    weight = jnp.exp2(score - peak)
+    latent_ref[...] = dot(weight.astype(jnp.bfloat16), draft)
+    peak_ref[...] = jnp.broadcast_to(peak, (ROWS, LANES))
+    total_ref[...] = jnp.broadcast_to(jnp.sum(weight, axis=1, keepdims=True), (ROWS, LANES))
+
+
+def attend_draft(own, draft_latent, draft_rope, tree):
+    vmem = pl.BlockSpec(memory_space=pltpu.VMEM)
+    return pl.pallas_call(
+        draft_kernel,
+        out_shape=[
+            jax.ShapeDtypeStruct((ROWS, LATENT), jnp.float32),
+            jax.ShapeDtypeStruct((ROWS, LANES), jnp.float32),
+            jax.ShapeDtypeStruct((ROWS, LANES), jnp.float32),
+        ],
+        in_specs=[vmem] * 4,
+        out_specs=[vmem] * 3,
+        compiler_params=pltpu.CompilerParams(vmem_limit_bytes=8 * 2**20),
+        cost_estimate=pl.CostEstimate(flops=10**9, bytes_accessed=2**20, transcendentals=0),
+        name="draft",
+    )(own, draft_latent, draft_rope, tree)
+
+
+def finish_kernel(tokens, heads, pieces_ref, d_lat_ref, d_peak_ref, d_total_ref, w_ref, out_ref):
+    n = pieces_ref.shape[0]
+    lses = []
+    for i in range(n):
+        parts = pieces_ref[i, 4 * ROWS :, :].astype(jnp.float32)
+        lses.append(parts[0:1, :] + parts[1:2, :] + parts[2:3, :])
     own_lane = lax.broadcasted_iota(jnp.int32, (ROWS, LANES), 1)
-    own_row = lax.broadcasted_iota(jnp.int32, (ROWS, LANES), 0)
-    diagonal = own_lane == own_row
-
-    def to_rows(line):
-        return jnp.sum(jnp.where(diagonal, line, 0.0), axis=1, keepdims=True)
-
-    cache_peak = to_rows(functools.reduce(jnp.maximum, lses))
-    peak = jnp.maximum(cache_peak, draft_peak)
-    weight = jnp.exp2(score - peak)
-    total = jnp.sum(weight, axis=1, keepdims=True)
-    latent = dot(weight.astype(jnp.bfloat16), draft)
-    for piece, lse in zip(pieces, lses):
-        share = jnp.exp2(to_rows(lse) - peak)
-        total = total + share
-        piece = jnp.concatenate([piece[j * ROWS : (j + 1) * ROWS, :] for j in range(4)], axis=1)
-        latent = latent + share * piece.astype(jnp.float32)
+    diagonal = own_lane == lax.broadcasted_iota(jnp.int32, (ROWS, LANES), 0)
+    draft_peak = d_peak_ref[:, :1]
+    lses = [jnp.sum(jnp.where(diagonal, lse, 0.0), axis=1, keepdims=True) for lse in lses]
+    peak = functools.reduce(jnp.maximum, lses, draft_peak)
+    keep = jnp.exp2(draft_peak - peak)
+    shares = [jnp.exp2(lse - peak) for lse in lses]
+    total = d_total_ref[:, :1] * keep + sum(shares[1:], shares[0])
+    latent = d_lat_ref[...] * keep
+    for i in range(n):
+        piece = [pieces_ref[i, j * ROWS : (j + 1) * ROWS, :] for j in range(4)]
+        latent = latent + shares[i] * jnp.concatenate(piece, axis=1).astype(jnp.float32)
     latent = latent / total
     high = latent.astype(jnp.bfloat16)
     low = (latent - high.astype(jnp.float32)).astype(jnp.bfloat16)
@@ -310,16 +329,16 @@
         out_ref[t] = value[t * heads : (t + 1) * heads, :].astype(out_ref.dtype)
 
 
-def finish(pieces, own, draft_latent, draft_rope, tree, w_value, tokens, heads):
+def finish(pieces, draft, w_value, tokens, heads):
     vmem = pl.BlockSpec(memory_space=pltpu.VMEM)
     return pl.pallas_call(
         functools.partial(finish_kernel, tokens, heads),
         out_shape=jax.ShapeDtypeStruct((tokens, heads, VDIM), jnp.bfloat16),
-        in_specs=[vmem] * 6,
+        in_specs=[vmem] * 5,
         out_specs=vmem,
         compiler_params=pltpu.CompilerParams(vmem_limit_bytes=8 * 2**20),
         name="finish",
-    )(pieces, own, draft_latent, draft_rope, tree, w_value)
+    )(pieces, *draft, w_value)
 
 
 def both_ways(n, step):
@@ -396,7 +415,8 @@
     pieces = lax.all_to_all(pieces, "z", 0, 0, tiled=True)
     tree = lax.dynamic_slice_in_dim(ancestors, lax.axis_index(BLK) * tokens, tokens, 0)
     tree = jnp.repeat(tree, heads, axis=0)
-    attended = finish(pieces, packed, draft_latent, draft_rope, tree, w_value, tokens, heads)
+    draft = attend_draft(packed, draft_latent, draft_rope, tree)
+    attended = finish(pieces, draft, w_value, tokens, heads)
     return (attended, counts[1, 0].astype(jnp.int32))
 
 

time: 107 us -> 107 us (level)
  the two profiles are of different devices: /device:TPU:4 before, /device:TPU:2 now
where the time goes in v3:
time: 107 us; the launch traced here: 106 us
  starting transfers between devices  42.2 us (39%)
  waiting for transfers between devices  42.1 us (39%)
  Pallas kernels  17.7 us (17%)
  between operations  3.24 us (3%)
  local copies, waits for them, and re-layouts  1.28 us (1%)
    ppermute x7, waiting for transfers between devices, shift(): lax.ppermute(value, (axis, 'core'), both_ways(lax.axis_size(axis), step))  20.4 us
    all_to_all x1, starting transfers between devices, shards(): pieces = lax.all_to_all(pieces, 'z', 0, 0, tiled=True)  13.9 us
    pallas_call x4, Pallas kernels, attend(): pl.pallas_call(functools.partial(attend_kernel, len(queries), n, counted)...  13.1 us
    ppermute x3, starting transfers between devices, rotate(): return lax.ppermute(value, axis, [(i, (i + step) % n) for i in range(n)])  12.6 us
    ppermute x7, starting transfers between devices, shift(): lax.ppermute(value, (axis, 'core'), both_ways(lax.axis_size(axis), step))  8.82 us
    all_to_all x1, waiting for transfers between devices, shards(): pieces = lax.all_to_all(pieces, 'z', 0, 0, tiled=True)  8.36 us
    ppermute x3, waiting for transfers between devices, rotate(): return lax.ppermute(value, axis, [(i, (i + step) % n) for i in range(n)])  6.27 us
    ppermute x2, waiting for transfers between devices, across(): return lax.ppermute(value, axis, [(i, (i + n // 2) % n) for i in range(n)])  4.93 us
  transfers between devices with their start and end apart: 18, of which 9 were waited for; matrix products, arithmetic and copies ran while one was open for 1% of the time, Pallas kernels for 13%

profile of v3, /device:TPU:2, one launch (start us, length us, event | category | flops | bytes accessed | tf_op | source)
XLA Modules:
  0.0 106.5 jit_solution(9561862442641100818)
XLA Ops:
  1.3 1.9 %pack_cache.1.refs_1_ = bf16[584,512]{1,0:T(8,128)(2,1)} custom-call(s32[1]{0:T(128)} %bitcast.4.valid, s32[8]{0:T(128)} %accepted.1, bf16[512,512]{1,0:T(8,128)(2,1)} %lat.1, bf16[64,512]{1,0:T(8,128)(2,1)} %rope.1), custom_call_target="tpu_custom_call" | custom-call | tf_op jit(solution)/shard_map/pack_cache/pallas_call | solution.py:255
  3.3 1.6 %collective-permute-start.4 = (bf16[584,512]{1,0:T(8,128)(2,1)}, bf16[584,512]{1,0:T(8,128)(2,1)S(1)}, u32[]{:S(2)}, u32[]{:S(2)}) collective-permute-start(bf16[584,512]{1,0:T(8,128)(2,1)} %pack_cache.1.refs_1_), channel_id=1, source_target_pairs={{0,2},{1,7},{2,4},{3,1},{4,6},{5,3},{6,0},{7,5},{8,10},{9,15},{10,... | collective-permute-start | bytes 1794056 | tf_op jit(solution)/shard_map/ppermute | solution.py:353
  4.8 0.8 collective-permute-start.5
  5.7 14.4 %collective-permute-done.4.refs_2_ = bf16[584,512]{1,0:T(8,128)(2,1)S(1)} collective-permute-done((bf16[584,512]{1,0:T(8,128)(2,1)}, bf16[584,512]{1,0:T(8,128)(2,1)S(1)}, u32[]{:S(2)}, u32[]{:S(2)}) %collective-permute-start.4) | collective-permute-done | bytes 598048 | tf_op jit(solution)/shard_map/ppermute | solution.py:353
  20.1 0.4 collective-permute-start.6
  20.6 2.0 %collective-permute-start = (bf16[1,144,128]{2,1,0:T(8,128)(2,1)S(1)}, bf16[1,144,128]{2,1,0:T(8,128)(2,1)S(1)}, u32[]{:S(2)}, u32[]{:S(2)}) collective-permute-start(bf16[1,144,128]{2,1,0:T(8,128)(2,1)S(1)} %pack_query.1.q_ref), channel_id=1, source_target_pairs={{0,32},{32,0},{64,96},{96,64},{128,160},{160,128},{192,224},{224,1... | collective-permute-start | bytes 110600 | tf_op jit(solution)/shard_map/ppermute | solution.py:362
  22.6 2.1 %collective-permute-done = bf16[1,144,128]{2,1,0:T(8,128)(2,1)S(1)} collective-permute-done((bf16[1,144,128]{2,1,0:T(8,128)(2,1)S(1)}, bf16[1,144,128]{2,1,0:T(8,128)(2,1)S(1)}, u32[]{:S(2)}, u32[]{:S(2)}) %collective-permute-start) | collective-permute-done | bytes 36896 | tf_op jit(solution)/shard_map/ppermute | solution.py:362
  24.8 3.3 %collective-permute-start.1 = (bf16[2,144,128]{2,1,0:T(8,128)(2,1)S(1)}, bf16[2,144,128]{2,1,0:T(8,128)(2,1)S(1)}, u32[]{:S(2)}, u32[]{:S(2)}) collective-permute-start(bf16[2,144,128]{2,1,0:T(8,128)(2,1)S(1)} %pad_maximum_fusion), channel_id=1, source_target_pairs={{0,64},{32,96},{64,128},{96,160},{128,192},{160,224},{192,0},{224,... | collective-permute-start | bytes 221192 | tf_op jit(solution)/shard_map/ppermute | solution.py:367
  28.1 5.3 %collective-permute-start.2 = (bf16[2,144,128]{2,1,0:T(8,128)(2,1)S(1)}, bf16[2,144,128]{2,1,0:T(8,128)(2,1)S(1)}, u32[]{:S(2)}, u32[]{:S(2)}) collective-permute-start(bf16[2,144,128]{2,1,0:T(8,128)(2,1)S(1)} %pad_maximum_fusion), channel_id=1, source_target_pairs={{0,128},{32,160},{64,192},{96,224},{128,0},{160,32},{192,64},{224,... | collective-permute-start | bytes 221192 | tf_op jit(solution)/shard_map/ppermute | solution.py:367
  33.4 0.5 collective-permute-done.1
  33.9 0.5 collective-permute-start.9
  34.5 3.8 %collective-permute-done.2 = bf16[2,144,128]{2,1,0:T(8,128)(2,1)S(1)} collective-permute-done((bf16[2,144,128]{2,1,0:T(8,128)(2,1)S(1)}, bf16[2,144,128]{2,1,0:T(8,128)(2,1)S(1)}, u32[]{:S(2)}, u32[]{:S(2)}) %collective-permute-start.2) | collective-permute-done | bytes 73760 | tf_op jit(solution)/shard_map/ppermute | solution.py:367
  38.3 4.0 %collective-permute-start.3 = (bf16[2,144,128]{2,1,0:T(8,128)(2,1)S(1)}, bf16[2,144,128]{2,1,0:T(8,128)(2,1)S(1)}, u32[]{:S(2)}, u32[]{:S(2)}) collective-permute-start(bf16[2,144,128]{2,1,0:T(8,128)(2,1)S(1)} %pad_maximum_fusion), channel_id=1, source_target_pairs={{0,192},{32,224},{64,0},{96,32},{128,64},{160,96},{192,128},{224,1... | collective-permute-start | bytes 221192 | tf_op jit(solution)/shard_map/ppermute | solution.py:367
  42.3 2.0 %collective-permute-done.3 = bf16[2,144,128]{2,1,0:T(8,128)(2,1)S(1)} collective-permute-done((bf16[2,144,128]{2,1,0:T(8,128)(2,1)S(1)}, bf16[2,144,128]{2,1,0:T(8,128)(2,1)S(1)}, u32[]{:S(2)}, u32[]{:S(2)}) %collective-permute-start.3) | collective-permute-done | bytes 73760 | tf_op jit(solution)/shard_map/ppermute | solution.py:367
  44.3 3.1 %collective-permute-start.15 = (bf16[8,144,128]{2,1,0:T(8,128)(2,1)S(1)}, bf16[8,144,128]{2,1,0:T(8,128)(2,1)S(1)}, u32[]{:S(2)}, u32[]{:S(2)}) collective-permute-start(bf16[8,144,128]{2,1,0:T(8,128)(2,1)S(1)} %constant_dynamic-update-slice_fusion.refs_0_), channel_id=1, source_target_pairs={{0,24},{1,9},{8,0},{9,17},{16,8},{17,25},{24,16},{25,1},{2,26},{3,... | collective-permute-start | bytes 884744 | tf_op jit(solution)/shard_map/ppermute | solution.py:353
  47.4 4.2 %collective-permute-done.15.refs_0_ = bf16[8,144,128]{2,1,0:T(8,128)(2,1)S(1)} collective-permute-done((bf16[8,144,128]{2,1,0:T(8,128)(2,1)S(1)}, bf16[8,144,128]{2,1,0:T(8,128)(2,1)S(1)}, u32[]{:S(2)}, u32[]{:S(2)}) %collective-permute-start.15) | collective-permute-done | bytes 294944 | tf_op jit(solution)/shard_map/ppermute | solution.py:353
  51.7 1.0 collective-permute-start.13
  52.7 4.1 %collective-permute-start.11 = (bf16[8,144,128]{2,1,0:T(8,128)(2,1)S(1)}, bf16[8,144,128]{2,1,0:T(8,128)(2,1)S(1)}, u32[]{:S(2)}, u32[]{:S(2)}) collective-permute-start(bf16[8,144,128]{2,1,0:T(8,128)(2,1)S(1)} %constant_dynamic-update-slice_fusion.refs_0_), channel_id=1, source_target_pairs={{0,16},{8,24},{16,0},{24,8},{1,17},{9,25},{17,1},{25,9},{2,18},{10... | collective-permute-start | bytes 884744 | tf_op jit(solution)/shard_map/ppermute | solution.py:358
  56.8 3.3 %attend.7 = bf16[8,136,128]{2,1,0:T(8,128)(2,1)S(1)} custom-call(bf16[8,144,128]{2,1,0:T(8,128)(2,1)S(1)} %collective-permute-done.15.refs_0_, bf16[584,512]{1,0:T(8,128)(2,1)S(1)} %copy-done.1, bf16[584,512]{1,0:T(8,128)(2,1)S(1)} %collective-permute-done.4.refs_2_, bf16[584,512]{1,0:T(8,128)(2,1)S(1)} %collective-permute-done.5.refs_3_, ...), custom_call_target="tpu_custom_call" | custom-call | flops 2684354560 | bytes 1048576 | tf_op jit(solution)/shard_map/attend/pallas_call | solution.py:124
  60.4 1.7 %collective-permute-done.13.refs_0_ = bf16[8,144,128]{2,1,0:T(8,128)(2,1)S(1)} collective-permute-done((bf16[8,144,128]{2,1,0:T(8,128)(2,1)S(1)}, bf16[8,144,128]{2,1,0:T(8,128)(2,1)S(1)}, u32[]{:S(2)}, u32[]{:S(2)}) %collective-permute-start.13) | collective-permute-done | bytes 294944 | tf_op jit(solution)/shard_map/ppermute | solution.py:353
  62.1 3.3 %attend.6 = bf16[8,136,128]{2,1,0:T(8,128)(2,1)S(1)} custom-call(bf16[8,144,128]{2,1,0:T(8,128)(2,1)S(1)} %collective-permute-done.13.refs_0_, bf16[584,512]{1,0:T(8,128)(2,1)S(1)} %copy-done.1, bf16[584,512]{1,0:T(8,128)(2,1)S(1)} %collective-permute-done.4.refs_2_, bf16[584,512]{1,0:T(8,128)(2,1)S(1)} %collective-permute-done.5.refs_3_, ...), custom_call_target="tpu_custom_call" | custom-call | flops 2684354560 | bytes 1048576 | tf_op jit(solution)/shard_map/attend/pallas_call | solution.py:124
  65.4 1.6 %collective-permute-start.14 = (bf16[8,136,128]{2,1,0:T(8,128)(2,1)S(1)}, bf16[8,136,128]{2,1,0:T(8,128)(2,1)S(1)}, u32[]{:S(2)}, u32[]{:S(2)}) collective-permute-start(bf16[8,136,128]{2,1,0:T(8,128)(2,1)S(1)} %attend.6), channel_id=1, source_target_pairs={{0,24},{1,9},{8,0},{9,17},{16,8},{17,25},{24,16},{25,1},{2,26},{3,... | collective-permute-start | bytes 835592 | tf_op jit(solution)/shard_map/ppermute | solution.py:353
  67.0 3.3 %attend.5 = (bf16[8,136,128]{2,1,0:T(8,128)(2,1)S(1)}, f32[8,128]{1,0:T(8,128)S(1)}) custom-call(bf16[8,144,128]{2,1,0:T(8,128)(2,1)S(1)} %collective-permute-done.11.refs_0_, bf16[584,512]{1,0:T(8,128)(2,1)S(1)} %copy-done.1, bf16[584,512]{1,0:T(8,128)(2,1)S(1)} %collective-permute-done.4.refs_2_, bf16[584,512]{1,0:T(8,128)(2,1)S(1)} %collective-permute-done.5.refs_3_, ...), custom_call_target="tpu_custom_call" | custom-call | flops 2684354560 | bytes 1048576 | tf_op jit(solution)/shard_map/attend/pallas_call | solution.py:124
  70.4 3.3 %attend.4.refs_0_ = bf16[8,136,128]{2,1,0:T(8,128)(2,1)S(1)} custom-call(bf16[8,144,128]{2,1,0:T(8,128)(2,1)S(1)} %constant_dynamic-update-slice_fusion.refs_0_, bf16[584,512]{1,0:T(8,128)(2,1)S(1)} %copy-done.1, bf16[584,512]{1,0:T(8,128)(2,1)S(1)} %collective-permute-done.4.refs_2_, bf16[584,512]{1,0:T(8,128)(2,1)S(1)} %collective-permute-done.5.refs_3_, ...), custom_call_target="tpu_custom_call" | custom-call | flops 2684354560 | bytes 1048576 | tf_op jit(solution)/shard_map/attend/pallas_call | solution.py:124
  73.8 4.9 %collective-permute-done.12.refs_1_ = bf16[8,136,128]{2,1,0:T(8,128)(2,1)S(1)} collective-permute-done((bf16[8,136,128]{2,1,0:T(8,128)(2,1)S(1)}, bf16[8,136,128]{2,1,0:T(8,128)(2,1)S(1)}, u32[]{:S(2)}, u32[]{:S(2)}) %collective-permute-start.12) | collective-permute-done | bytes 278560 | tf_op jit(solution)/shard_map/ppermute | solution.py:358
  78.7 1.0 merge.1
  79.7 13.9 %all-to-all-start = ((bf16[8,136,128]{2,1,0:T(8,128)(2,1)}), bf16[8,136,128]{2,1,0:T(8,128)(2,1)S(1)}, u32[]{:S(2)}, u32[]{:S(2)}) async-start(bf16[8,136,128]{2,1,0:T(8,128)(2,1)} %merge.1), calls=%async_computation | async-start | bytes 557056 | tf_op jit(solution)/shard_map/all_to_all | solution.py:415
  93.6 0.7 copy-done.6
  94.3 0.4 draft.1
  94.7 0.5 slice.3
  95.9 8.4 %all-to-all-done.pieces_ref = bf16[8,136,128]{2,1,0:T(8,128)(2,1)S(1)} async-done(((bf16[8,136,128]{2,1,0:T(8,128)(2,1)}), bf16[8,136,128]{2,1,0:T(8,128)(2,1)S(1)}, u32[]{:S(2)}, u32[]{:S(2)}) %all-to-all-start) | async-done | bytes 278560 | tf_op jit(solution)/shard_map/all_to_all | solution.py:415
  104.2 1.1 %finish.1 = bf16[8,4,128]{2,1,0:T(4,128)(2,1)} custom-call(bf16[8,136,128]{2,1,0:T(8,128)(2,1)S(1)} %all-to-all-done.pieces_ref, f32[32,512]{1,0:T(8,128)S(1)} %get-tuple-element.8.d_lat_ref, f32[32,128]{1,0:T(8,128)S(1)} %get-tuple-element.9.d_peak_ref, f32[32,128]{1,0:T(8,128)S(1)} %get-tuple-element.10.d_total_ref, bf16[4,512,128]{2,1,0:T(8,128)(2,1)S(1)} %copy-done.2), custom_call_target="tpu_custom_call" | custom-call | tf_op jit(solution)/shard_map/finish/pallas_call | solution.py:334
  (36 shorter events, 0.7 us)
Async XLA Ops:
  0.6 93.0 %copy-start = (s32[64,64]{1,0:T(8,128)S(1)}, s32[64,64]{1,0:T(8,128)}, u32[]{:S(2)}) copy-start(s32[64,64]{1,0:T(8,128)} %param.16) | copy-start | bytes 49156
  1.3 19.3 %copy-start.3 = (bf16[8,4,512]{2,1,0:T(4,128)(2,1)S(1)}, bf16[8,4,512]{2,1,0:T(4,128)(2,1)}, u32[]{:S(2)}) copy-start(bf16[8,4,512]{2,1,0:T(4,128)(2,1)} %lat_ref.1) | copy-start | bytes 98308
  1.3 19.2 %copy-start.4 = (bf16[8,64,4]{1,2,0:T(4,128)(2,1)S(1)}, bf16[8,64,4]{1,2,0:T(4,128)(2,1)}, u32[]{:S(2)}) copy-start(bf16[8,64,4]{1,2,0:T(4,128)(2,1)} %param.11) | copy-start | bytes 12292
  3.3 53.6 %copy-start.1 = (bf16[584,512]{1,0:T(8,128)(2,1)S(1)}, bf16[584,512]{1,0:T(8,128)(2,1)}, u32[]{:S(2)}) copy-start(bf16[584,512]{1,0:T(8,128)(2,1)} %pack_cache.1.refs_1_) | copy-start | bytes 1794052
  3.3 16.8 %collective-permute-start.4 = (bf16[584,512]{1,0:T(8,128)(2,1)}, bf16[584,512]{1,0:T(8,128)(2,1)S(1)}, u32[]{:S(2)}, u32[]{:S(2)}) collective-permute-start(bf16[584,512]{1,0:T(8,128)(2,1)} %pack_cache.1.refs_1_), channel_id=1, source_target_pairs={{0,2},{1,7},{2,4},{3,1},{4,6},{5,3},{6,0},{7,5},{8,10},{9,15},{10,... | collective-permute-start | bytes 1794056 | tf_op jit(solution)/shard_map/ppermute | solution.py:353
  4.8 29.1 %collective-permute-start.5 = (bf16[584,512]{1,0:T(8,128)(2,1)}, bf16[584,512]{1,0:T(8,128)(2,1)S(1)}, u32[]{:S(2)}, u32[]{:S(2)}) collective-permute-start(bf16[584,512]{1,0:T(8,128)(2,1)} %pack_cache.1.refs_1_), channel_id=1, source_target_pairs={{0,6},{1,3},{2,0},{3,5},{4,2},{5,7},{6,4},{7,1},{8,14},{9,11},{10,... | collective-permute-start | bytes 1794056 | tf_op jit(solution)/shard_map/ppermute | solution.py:353
  20.1 14.3 %collective-permute-start.6 = (bf16[584,512]{1,0:T(8,128)(2,1)S(1)}, bf16[584,512]{1,0:T(8,128)(2,1)S(1)}, u32[]{:S(2)}, u32[]{:S(2)}) collective-permute-start(bf16[584,512]{1,0:T(8,128)(2,1)S(1)} %collective-permute-done.4.refs_2_), channel_id=1, source_target_pairs={{0,2},{1,7},{2,4},{3,1},{4,6},{5,3},{6,0},{7,5},{8,10},{9,15},{10,... | collective-permute-start | bytes 1794056 | tf_op jit(solution)/shard_map/ppermute | solution.py:353
  20.5 32.2 %collective-permute-start.7 = (bf16[584,512]{1,0:T(8,128)(2,1)}, bf16[584,512]{1,0:T(8,128)(2,1)S(1)}, u32[]{:S(2)}, u32[]{:S(2)}) collective-permute-start(bf16[584,512]{1,0:T(8,128)(2,1)} %pack_cache.1.refs_1_), channel_id=1, source_target_pairs={{0,1},{1,0},{2,3},{3,2},{4,5},{5,4},{6,7},{7,6},{8,9},{9,8},{10,11... | collective-permute-start | bytes 1794056 | tf_op jit(solution)/shard_map/ppermute | solution.py:371
  20.6 4.1 %collective-permute-start = (bf16[1,144,128]{2,1,0:T(8,128)(2,1)S(1)}, bf16[1,144,128]{2,1,0:T(8,128)(2,1)S(1)}, u32[]{:S(2)}, u32[]{:S(2)}) collective-permute-start(bf16[1,144,128]{2,1,0:T(8,128)(2,1)S(1)} %pack_query.1.q_ref), channel_id=1, source_target_pairs={{0,32},{32,0},{64,96},{96,64},{128,160},{160,128},{192,224},{224,1... | collective-permute-start | bytes 110600 | tf_op jit(solution)/shard_map/ppermute | solution.py:362
  24.8 9.2 %collective-permute-start.1 = (bf16[2,144,128]{2,1,0:T(8,128)(2,1)S(1)}, bf16[2,144,128]{2,1,0:T(8,128)(2,1)S(1)}, u32[]{:S(2)}, u32[]{:S(2)}) collective-permute-start(bf16[2,144,128]{2,1,0:T(8,128)(2,1)S(1)} %pad_maximum_fusion), channel_id=1, source_target_pairs={{0,64},{32,96},{64,128},{96,160},{128,192},{160,224},{192,0},{224,... | collective-permute-start | bytes 221192 | tf_op jit(solution)/shard_map/ppermute | solution.py:367
  28.1 10.2 %collective-permute-start.2 = (bf16[2,144,128]{2,1,0:T(8,128)(2,1)S(1)}, bf16[2,144,128]{2,1,0:T(8,128)(2,1)S(1)}, u32[]{:S(2)}, u32[]{:S(2)}) collective-permute-start(bf16[2,144,128]{2,1,0:T(8,128)(2,1)S(1)} %pad_maximum_fusion), channel_id=1, source_target_pairs={{0,128},{32,160},{64,192},{96,224},{128,0},{160,32},{192,64},{224,... | collective-permute-start | bytes 221192 | tf_op jit(solution)/shard_map/ppermute | solution.py:367
  33.9 22.9 %collective-permute-start.8 = (bf16[584,512]{1,0:T(8,128)(2,1)S(1)}, bf16[584,512]{1,0:T(8,128)(2,1)S(1)}, u32[]{:S(2)}, u32[]{:S(2)}) collective-permute-start(bf16[584,512]{1,0:T(8,128)(2,1)S(1)} %collective-permute-done.4.refs_2_), channel_id=1, source_target_pairs={{0,1},{1,0},{2,3},{3,2},{4,5},{5,4},{6,7},{7,6},{8,9},{9,8},{10,11... | collective-permute-start | bytes 1794056 | tf_op jit(solution)/shard_map/ppermute | solution.py:371
  33.9 22.9 %collective-permute-start.9 = (bf16[584,512]{1,0:T(8,128)(2,1)S(1)}, bf16[584,512]{1,0:T(8,128)(2,1)S(1)}, u32[]{:S(2)}, u32[]{:S(2)}) collective-permute-start(bf16[584,512]{1,0:T(8,128)(2,1)S(1)} %collective-permute-done.5.refs_3_), channel_id=1, source_target_pairs={{0,1},{1,0},{2,3},{3,2},{4,5},{5,4},{6,7},{7,6},{8,9},{9,8},{10,11... | collective-permute-start | bytes 1794056 | tf_op jit(solution)/shard_map/ppermute | solution.py:371
  34.4 22.4 %collective-permute-start.10 = (bf16[584,512]{1,0:T(8,128)(2,1)S(1)}, bf16[584,512]{1,0:T(8,128)(2,1)S(1)}, u32[]{:S(2)}, u32[]{:S(2)}) collective-permute-start(bf16[584,512]{1,0:T(8,128)(2,1)S(1)} %collective-permute-done.6.refs_4_), channel_id=1, source_target_pairs={{0,1},{1,0},{2,3},{3,2},{4,5},{5,4},{6,7},{7,6},{8,9},{9,8},{10,11... | collective-permute-start | bytes 1794056 | tf_op jit(solution)/shard_map/ppermute | solution.py:371
  38.3 6.0 %collective-permute-start.3 = (bf16[2,144,128]{2,1,0:T(8,128)(2,1)S(1)}, bf16[2,144,128]{2,1,0:T(8,128)(2,1)S(1)}, u32[]{:S(2)}, u32[]{:S(2)}) collective-permute-start(bf16[2,144,128]{2,1,0:T(8,128)(2,1)S(1)} %pad_maximum_fusion), channel_id=1, source_target_pairs={{0,192},{32,224},{64,0},{96,32},{128,64},{160,96},{192,128},{224,1... | collective-permute-start | bytes 221192 | tf_op jit(solution)/shard_map/ppermute | solution.py:367
  44.3 7.3 %collective-permute-start.15 = (bf16[8,144,128]{2,1,0:T(8,128)(2,1)S(1)}, bf16[8,144,128]{2,1,0:T(8,128)(2,1)S(1)}, u32[]{:S(2)}, u32[]{:S(2)}) collective-permute-start(bf16[8,144,128]{2,1,0:T(8,128)(2,1)S(1)} %constant_dynamic-update-slice_fusion.refs_0_), channel_id=1, source_target_pairs={{0,24},{1,9},{8,0},{9,17},{16,8},{17,25},{24,16},{25,1},{2,26},{3,... | collective-permute-start | bytes 884744 | tf_op jit(solution)/shard_map/ppermute | solution.py:353
  51.7 10.5 %collective-permute-start.13 = (bf16[8,144,128]{2,1,0:T(8,128)(2,1)S(1)}, bf16[8,144,128]{2,1,0:T(8,128)(2,1)S(1)}, u32[]{:S(2)}, u32[]{:S(2)}) collective-permute-start(bf16[8,144,128]{2,1,0:T(8,128)(2,1)S(1)} %constant_dynamic-update-slice_fusion.refs_0_), channel_id=1, source_target_pairs={{0,8},{1,25},{8,16},{9,1},{16,24},{17,9},{24,0},{25,17},{2,10},{3,... | collective-permute-start | bytes 884744 | tf_op jit(solution)/shard_map/ppermute | solution.py:353
  52.7 14.3 %collective-permute-start.11 = (bf16[8,144,128]{2,1,0:T(8,128)(2,1)S(1)}, bf16[8,144,128]{2,1,0:T(8,128)(2,1)S(1)}, u32[]{:S(2)}, u32[]{:S(2)}) collective-permute-start(bf16[8,144,128]{2,1,0:T(8,128)(2,1)S(1)} %constant_dynamic-update-slice_fusion.refs_0_), channel_id=1, source_target_pairs={{0,16},{8,24},{16,0},{24,8},{1,17},{9,25},{17,1},{25,9},{2,18},{10... | collective-permute-start | bytes 884744 | tf_op jit(solution)/shard_map/ppermute | solution.py:358
  60.1 13.6 %collective-permute-start.16 = (bf16[8,136,128]{2,1,0:T(8,128)(2,1)S(1)}, bf16[8,136,128]{2,1,0:T(8,128)(2,1)S(1)}, u32[]{:S(2)}, u32[]{:S(2)}) collective-permute-start(bf16[8,136,128]{2,1,0:T(8,128)(2,1)S(1)} %attend.7), channel_id=1, source_target_pairs={{0,8},{1,25},{8,16},{9,1},{16,24},{17,9},{24,0},{25,17},{2,10},{3,... | collective-permute-start | bytes 835592 | tf_op jit(solution)/shard_map/ppermute | solution.py:353
  65.4 8.3 %collective-permute-start.14 = (bf16[8,136,128]{2,1,0:T(8,128)(2,1)S(1)}, bf16[8,136,128]{2,1,0:T(8,128)(2,1)S(1)}, u32[]{:S(2)}, u32[]{:S(2)}) collective-permute-start(bf16[8,136,128]{2,1,0:T(8,128)(2,1)S(1)} %attend.6), channel_id=1, source_target_pairs={{0,24},{1,9},{8,0},{9,17},{16,8},{17,25},{24,16},{25,1},{2,26},{3,... | collective-permute-start | bytes 835592 | tf_op jit(solution)/shard_map/ppermute | solution.py:353
  70.3 8.4 %collective-permute-start.12 = (bf16[8,136,128]{2,1,0:T(8,128)(2,1)S(1)}, bf16[8,136,128]{2,1,0:T(8,128)(2,1)S(1)}, u32[]{:S(2)}, u32[]{:S(2)}) collective-permute-start(bf16[8,136,128]{2,1,0:T(8,128)(2,1)S(1)} %get-tuple-element.7), channel_id=1, source_target_pairs={{0,16},{8,24},{16,0},{24,8},{1,17},{9,25},{17,1},{25,9},{2,18},{10... | collective-permute-start | bytes 835592 | tf_op jit(solution)/shard_map/ppermute | solution.py:358
  79.7 13.9 %copy-start.5 = (bf16[64,512]{1,0:T(8,128)(2,1)S(1)}, bf16[64,512]{1,0:T(8,128)(2,1)}, u32[]{:S(2)}) copy-start(bf16[64,512]{1,0:T(8,128)(2,1)} %d_lat_ref.1) | copy-start | bytes 196612
  79.7 24.5 %all-to-all-start = ((bf16[8,136,128]{2,1,0:T(8,128)(2,1)}), bf16[8,136,128]{2,1,0:T(8,128)(2,1)S(1)}, u32[]{:S(2)}, u32[]{:S(2)}) async-start(bf16[8,136,128]{2,1,0:T(8,128)(2,1)} %merge.1), calls=%async_computation | async-start | bytes 557056 | tf_op jit(solution)/shard_map/all_to_all | solution.py:415
  93.6 0.7 copy-start.6
  94.3 9.9 %copy-start.2 = (bf16[4,512,128]{2,1,0:T(8,128)(2,1)S(1)}, bf16[4,512,128]{2,1,0:T(8,128)(2,1)}, u32[]{:S(2)}) copy-start(bf16[4,512,128]{2,1,0:T(8,128)(2,1)} %w_ref.1) | copy-start | bytes 1572868
